TPU v7x, 256 devices: a whole 4x4x8 slice. The times are simulated.
256 devices in a mesh: gx: 32 (over z, x), gy: 8 (over y, core).
Axes of the slice: x: 4, y: 4, z: 8, core: 2. Of those that a mesh axis runs over, the one named last changes fastest.
Arguments:
- velocity: float32 [2, 2048, 4096], P(None, 'gy', 'gx'), may hold values from -3 to 3
- stress: float32 [3, 2048, 4096], P(None, 'gy', 'gx'), may hold values from -3 to 3
- ice_mass: float32 [2048, 4096], P('gy', 'gx'), may hold values from 0.5 to 4
- strength: float32 [2048, 4096], P('gy', 'gx'), may hold values from 0.2 to 2
- land_mask: int32 [2048, 4096], P('gy', 'gx'), may hold values from 0 to 1
- ocean_forcing: float32 [4, 2048, 4096], P(None, ('gy', 'gx')), may hold values from -3 to 3
Outputs:
- velocity_out: float32 [2, 2048, 4096], P(None, 'gy', 'gx')
- stress_out: float32 [3, 2048, 4096], P(None, 'gy', 'gx')
- residuals: float32 [4], replicated
- ocean_stress: float32 [2, 2048, 4096], P(None, ('gy', 'gx'))
All inputs are finite; a program needn't handle non-finite values.
Results may differ from a plain program's by a relative error of at most 0.0001.
Values sent between devices are 32-bit elements; how exact they have to be, the bound alone decides.
A program may use at most 64 MiB of HBM per device.

v0:
```python
import jax
import jax.numpy as jnp
from jax import lax
from jax.sharding import Mesh
from jax.sharding import PartitionSpec as P

ITERS = 4
GX = ("gx_0", "gx_1")
GY = ("gy_0", "gy_1")
GX_GY = ("gx_0", "gx_1", "gy_0", "gy_1")
GY_GX = ("gy_0", "gy_1", "gx_0", "gx_1")


ALPHA = 4.0
BETA = 4.0
WATER_DRAG = 1.0
DELTA_FLOOR = 0.0025


def cut_along(array, dim, count):
    before, after = (array.shape[:dim], array.shape[dim + 1 :])
    return jnp.moveaxis(array.reshape(*before, count, -1, *after), dim, 0)


def joined_along(parts, dim):
    lengths = list(parts.shape[1:])
    lengths[dim] *= parts.shape[0]
    return jnp.moveaxis(parts, 0, dim).reshape(lengths)


def moved_by_axis(parts, axes, order):
    inside = parts.shape[1:]
    filled = parts.reshape(*(lax.axis_size(a) for a in axes), *inside)
    for k in order:
        filled = lax.all_to_all(filled, axes[k], k, k, tiled=True)
    return filled.reshape(-1, *inside)


def one_axis_at_a_time(array, axes, order, split_dim, concat_dim):
    parts = cut_along(array, split_dim, lax.axis_size(axes))
    return joined_along(moved_by_axis(parts, axes, order), concat_dim)


def extended(cells, sides, width):
    for axis, dim in sides:
        count = lax.axis_size(axis)
        head = lax.slice_in_dim(cells, 0, width, axis=dim)
        tail = lax.slice_in_dim(cells, cells.shape[dim] - width, cells.shape[dim], axis=dim)
        cells = jnp.concatenate(
            [
                lax.ppermute(tail, axis, [(i, (i + 1) % count) for i in range(count)]),
                cells,
                lax.ppermute(head, axis, [((i + 1) % count, i) for i in range(count)]),
            ],
            axis=dim,
        )
    return cells


def over_axes(array, axes):
    for axis in axes:
        array = lax.psum(array, axis)
    return array


def diff_east(padded):
    return 0.5 * (padded[..., 1:-1, 2:] - padded[..., 1:-1, :-2])


def diff_north(padded):
    return 0.5 * (padded[..., 2:, 1:-1] - padded[..., :-2, 1:-1])


def trim_edges(field, level):
    if level == 0:
        return field
    return field[..., level:-level, level:-level]


def record_sum(own_sum, local_sums):
    local_sums.append(own_sum)


def relax_stress(padded_vel, stress, strength, ice_frac):
    east_dx = diff_east(padded_vel[0])
    east_dy = diff_north(padded_vel[0])
    north_dx = diff_east(padded_vel[1])
    north_dy = diff_north(padded_vel[1])
    divergence = east_dx + north_dy
    tension = east_dx - north_dy
    shear_rate = east_dy + north_dx
    delta_rate = jnp.sqrt(
        divergence * divergence + 0.25 * (tension * tension + shear_rate * shear_rate) + DELTA_FLOOR
    )
    target = jnp.stack(
        [
            strength * (divergence / delta_rate - 1.0),
            strength * tension / (4.0 * delta_rate),
            strength * shear_rate / (8.0 * delta_rate),
        ]
    )
    return (stress + (target - stress) / ALPHA) * ice_frac


def drag_coeff(vel, currents):
    east_gap = currents[0] - vel[0]
    north_gap = currents[1] - vel[1]
    return WATER_DRAG * jnp.sqrt(east_gap * east_gap + north_gap * north_gap + 0.01)


def relax_velocity(padded_stress, vel, vel_start, forcing, ice_mass, coriolis, ice_frac):
    normal_xx = 0.5 * (padded_stress[0] + padded_stress[1])
    normal_yy = 0.5 * (padded_stress[0] - padded_stress[1])
    shear_xy = padded_stress[2]
    force_east = diff_east(normal_xx) + diff_north(shear_xy)
    force_north = diff_east(shear_xy) + diff_north(normal_yy)
    drag_rate = drag_coeff(vel, forcing[2:4])
    denominator = BETA + 1.0 + drag_rate / ice_mass
    new_east = (
        (
            BETA * vel[0]
            + vel_start[0]
            + (force_east + forcing[0] + drag_rate * forcing[2]) / ice_mass
            + coriolis * vel[1]
        )
        / denominator
        * ice_frac
    )
    new_north = (
        (
            BETA * vel[1]
            + vel_start[1]
            + (force_north + forcing[1] + drag_rate * forcing[3]) / ice_mass
            - coriolis * vel[0]
        )
        / denominator
        * ice_frac
    )
    return jnp.stack([new_east, new_north])


def local(velocity, stress, ice_mass, strength, land_mask, ocean_forcing):
    row_count = velocity.shape[1]
    col_count = velocity.shape[2]
    forcing = one_axis_at_a_time(ocean_forcing, GX, (0, 1), 2, 1)
    ice_frac = land_mask.astype(jnp.float32)
    lat_band = lax.axis_index(GY)
    total_rows = lax.axis_size(GY) * row_count
    local_sums = []
    depth = 2 * ITERS
    stacked = jnp.concatenate(
        [velocity, stress, strength[None], ice_mass[None], ice_frac[None], forcing], axis=0
    )
    padded = extended(stacked, ((GX, 2), (GY, 1)), depth)
    wide_rows = lat_band * row_count - depth + jnp.arange(row_count + 2 * depth, dtype=jnp.int32)
    inside = ((wide_rows >= 0) & (wide_rows < total_rows)).astype(jnp.float32)[:, None]
    wide_vel = padded[0:2] * inside
    wide_stress = padded[2:5] * inside
    wide_strength = padded[5]
    wide_mass = padded[6]
    wide_ice = padded[7] * inside
    wide_forcing = padded[8:12]
    wide_lat = wide_rows.astype(jnp.float32)
    wide_coriolis = jnp.broadcast_to(
        (0.3 + 1.2 * (wide_lat + 0.5) / total_rows)[:, None],
        (row_count + 2 * depth, col_count + 2 * depth),
    )
    vel_work = wide_vel
    stress_work = wide_stress
    margin = depth
    for subcycle in range(ITERS):
        level_one = depth - (margin - 1)
        stress_cut = (stress_work.shape[-1] - (col_count + 2 * (margin - 1))) // 2
        stress_work = relax_stress(
            vel_work,
            trim_edges(stress_work, stress_cut),
            trim_edges(wide_strength, level_one),
            trim_edges(wide_ice, level_one),
        )
        level_two = depth - (margin - 2)
        old_vel = trim_edges(vel_work, 2)
        new_vel = relax_velocity(
            stress_work,
            old_vel,
            trim_edges(wide_vel, level_two),
            trim_edges(wide_forcing, level_two),
            trim_edges(wide_mass, level_two),
            trim_edges(wide_coriolis, level_two),
            trim_edges(wide_ice, level_two),
        )
        change = trim_edges(new_vel - old_vel, margin - 2)
        record_sum(jnp.sum(change * change), local_sums)
        vel_work = new_vel
        margin = margin - 2
    stress = trim_edges(stress_work, 1)
    history = over_axes(jnp.stack(local_sums), GX_GY)
    drag_rate = drag_coeff(vel_work, forcing[2:4])
    ice_stress = drag_rate * (vel_work - forcing[2:4]) * ice_frac
    ocean_stress = lax.all_to_all(ice_stress, GX, split_axis=1, concat_axis=2, tiled=True)
    return (vel_work, stress, history, ocean_stress)


def solution(mesh):
    torus = Mesh(mesh.devices.reshape(8, 4, 4, 2), ("gx_0", "gx_1", "gy_0", "gy_1"))
    placed = (
        P(None, GY, GX),
        P(None, GY, GX),
        P(GY, GX),
        P(GY, GX),
        P(GY, GX),
        P(None, GY_GX, None),
    )
    return jax.shard_map(
        local,
        mesh=torus,
        in_specs=placed,
        out_specs=(P(None, GY, GX), P(None, GY, GX), P(), P(None, GY_GX, None)),
        check_vma=False,
    )
```

profile of v0, /device:TPU:1, one launch (start us, length us, event | category | flops | bytes accessed | tf_op | source)
XLA Modules:
  0.0 139.0 jit_solution(16432302177492272811)
XLA Ops:
  0.6 1.2 copy.50
  1.8 1.1 copy.32
  3.0 9.1 %all-to-all-start = ((f32[8,4,4,8,128]{4,3,1,2,0:T(8,128)}), f32[8,4,4,8,128]{4,3,1,2,0:T(8,128)S(1)}, u32[]{:S(2)}, u32[]{:S(2)}) async-start(f32[8,4,4,8,128]{4,3,1,2,0:T(8,128)} %copy.32), calls=%async_computation | async-start | bytes 1048576 | tf_op jit(solution)/shard_map/all_to_all | solution.py:35
  12.3 17.8 %all-to-all-done = f32[8,4,4,8,128]{4,3,1,2,0:T(8,128)S(1)} async-done(((f32[8,4,4,8,128]{4,3,1,2,0:T(8,128)}), f32[8,4,4,8,128]{4,3,1,2,0:T(8,128)S(1)}, u32[]{:S(2)}, u32[]{:S(2)}) %all-to-all-start) | async-done | bytes 524320 | tf_op jit(solution)/shard_map/all_to_all | solution.py:35
  30.9 4.0 %all-to-all-start.1 = ((f32[8,4,4,8,128]{4,3,0,2,1:T(8,128)}), f32[8,4,4,8,128]{4,3,0,2,1:T(8,128)S(1)}, u32[]{:S(2)}, u32[]{:S(2)}) async-start(f32[8,4,4,8,128]{4,3,0,2,1:T(8,128)} %copy.33), calls=%async_computation.1 | async-start | bytes 1048576 | tf_op jit(solution)/shard_map/all_to_all | solution.py:35
  35.1 8.6 %all-to-all-done.1 = f32[8,4,4,8,128]{4,3,0,2,1:T(8,128)S(1)} async-done(((f32[8,4,4,8,128]{4,3,0,2,1:T(8,128)}), f32[8,4,4,8,128]{4,3,0,2,1:T(8,128)S(1)}, u32[]{:S(2)}, u32[]{:S(2)}) %all-to-all-start.1) | async-done | bytes 524320 | tf_op jit(solution)/shard_map/all_to_all | solution.py:35
  44.6 1.7 %fusion.150 = (f32[12,256,8]{2,1,0:T(8,128)}, f32[12,256,8]{2,1,0:T(8,128)S(1)}) fusion(f32[12,256,128]{2,1,0:T(8,128)S(1)} %bitcast_dynamic-update-slice_fusion), kind=kLoop, calls=%fused_computation.281 | loop fusion | bytes 393216 | tf_op jit(solution)/shard_map/slice | solution.py:48
  46.3 1.8 %copy.36 = f32[12,256,8]{1,2,0:T(8,128)S(1)} copy(f32[12,256,8]{2,1,0:T(8,128)} %get-tuple-element.37) | data formatting | bytes 196608 | tf_op jit(solution)/shard_map/slice | solution.py:48
  49.6 4.5 %collective-permute-start.1 = (f32[12,256,8]{1,2,0:T(8,128)}, f32[12,256,8]{1,2,0:T(8,128)}, u32[]{:S(2)}, u32[]{:S(2)}) collective-permute-start(f32[12,256,8]{1,2,0:T(8,128)} %copy.37), channel_id=1, source_target_pairs={{8,0},{16,8},{24,16},{32,24},{40,32},{48,40},{56,48},{64,56},{72,6... | collective-permute-start | bytes 294920 | tf_op jit(solution)/shard_map/ppermute | solution.py:53
  56.0 2.5 %copy.39 = f32[12,256,8]{2,1,0:T(8,128)} copy(f32[12,256,8]{1,2,0:T(8,128)} %collective-permute-done.1) | data formatting | bytes 196608 | tf_op jit(solution)/shard_map/ppermute | solution.py:53
  58.5 1.1 pad_maximum_fusion.7
  59.6 4.0 %collective-permute-start.2 = (f32[12,8,144]{2,1,0:T(8,128)S(1)}, f32[12,8,144]{2,1,0:T(8,128)S(1)}, u32[]{:S(2)}, u32[]{:S(2)}) collective-permute-start(f32[12,8,144]{2,1,0:T(8,128)S(1)} %get-tuple-element.33), channel_id=1, source_target_pairs={{0,1},{1,2},{2,3},{3,4},{4,5},{5,6},{6,7},{7,0},{8,9},{9,10},{10,1... | collective-permute-start | bytes 165896 | tf_op jit(solution)/shard_map/ppermute | solution.py:51
  63.7 1.5 %collective-permute-done.2 = f32[12,8,144]{2,1,0:T(8,128)S(1)} collective-permute-done((f32[12,8,144]{2,1,0:T(8,128)S(1)}, f32[12,8,144]{2,1,0:T(8,128)S(1)}, u32[]{:S(2)}, u32[]{:S(2)}) %collective-permute-start.2) | collective-permute-done | bytes 55328 | tf_op jit(solution)/shard_map/ppermute | solution.py:51
  65.2 2.4 %collective-permute-done.3 = f32[12,8,144]{2,1,0:T(8,128)S(1)} collective-permute-done((f32[12,8,144]{2,1,0:T(8,128)S(1)}, f32[12,8,144]{2,1,0:T(8,128)S(1)}, u32[]{:S(2)}, u32[]{:S(2)}) %collective-permute-start.3) | collective-permute-done | bytes 55328 | tf_op jit(solution)/shard_map/ppermute | solution.py:53
  67.6 1.3 pad_maximum_fusion
  72.9 1.5 %copy-done.1 = f32[12,272,144]{2,1,0:T(8,128)S(1)} copy-done((f32[12,272,144]{2,1,0:T(8,128)S(1)}, f32[12,272,144]{2,1,0:T(8,128)}, u32[]{:S(2)}) %copy-start.1) | copy-done | bytes 1880088
  81.5 1.1 fusion.48
  86.0 7.1 %all-to-all-start.2 = ((f32[2,256,128]{2,0,1:T(2,128)}), f32[2,256,128]{2,0,1:T(2,128)S(1)}, u32[]{:S(2)}, u32[]{:S(2)}) async-start(f32[2,256,128]{2,0,1:T(2,128)} %copy.41), calls=%async_computation.2 | async-start | bytes 524288 | tf_op jit(solution)/shard_map/all_to_all | solution.py:199
  93.3 1.2 fusion.98
  94.6 2.7 %pad_maximum_fusion.8 = f32[4]{0:T(128)S(1)} fusion(f32[1]{0:T(128)} %bitcast.80, f32[1]{0:T(128)} %bitcast.79, f32[1]{0:T(128)} %bitcast.78, f32[1]{0:T(128)} %bitcast.77), kind=kLoop, calls=%fused_computation.280 | loop fusion | flops 12 | bytes 32 | tf_op jit(solution)/shard_map/stack | solution.py:196
  97.3 13.8 %psum.28 = f32[4]{0:T(128)S(1)} all-reduce(f32[4]{0:T(128)S(1)} %pad_maximum_fusion.8), channel_id=1, replica_groups=mesh['gx_0'=8,'gx_1'=4,'gy_0'=4,'gy_1'=2] {'gx_0'}, use_global_device_ids=true, to_apply=%region_4.0 | all-reduce | flops 4 | bytes 32 | tf_op jit(solution)/shard_map/psum | solution.py:62
  111.0 8.4 %psum.29 = f32[4]{0:T(128)S(1)} all-reduce(f32[4]{0:T(128)S(1)} %psum.28), channel_id=1, replica_groups=mesh['gx_0'=8,'gx_1'=4,'gy_0'=4,'gy_1'=2] {'gx_1'}, use_global_device_ids=true, to_apply=%region_5.0 | all-reduce | flops 4 | bytes 32 | tf_op jit(solution)/shard_map/psum | solution.py:62
  119.4 8.3 %psum.30 = f32[4]{0:T(128)S(1)} all-reduce(f32[4]{0:T(128)S(1)} %psum.29), channel_id=1, replica_groups=mesh['gx_0'=8,'gx_1'=4,'gy_0'=4,'gy_1'=2] {'gy_0'}, use_global_device_ids=true, to_apply=%region_6.0 | all-reduce | flops 4 | bytes 32 | tf_op jit(solution)/shard_map/psum | solution.py:62
  127.7 9.7 %psum.31 = f32[4]{0:T(128)} all-reduce(f32[4]{0:T(128)S(1)} %psum.30), channel_id=1, replica_groups=mesh['gx_0'=8,'gx_1'=4,'gy_0'=4,'gy_1'=2] {'gy_1'}, use_global_device_ids=true, to_apply=%region_7.0 | all-reduce | flops 4 | bytes 32 | tf_op jit(solution)/shard_map/psum | solution.py:62
  (80 shorter events, 21.7 us)
Async XLA Ops:
  0.6 11.5 %copy-start.8 = (f32[2,256,128]{2,1,0:T(8,128)S(1)}, f32[2,256,128]{2,1,0:T(8,128)}, u32[]{:S(2)}) copy-start(f32[2,256,128]{2,1,0:T(8,128)} %param.6) | copy-start | bytes 786436
  1.8 10.3 %copy-start.7 = (f32[3,256,128]{2,1,0:T(8,128)S(1)}, f32[3,256,128]{2,1,0:T(8,128)}, u32[]{:S(2)}) copy-start(f32[3,256,128]{2,1,0:T(8,128)} %param.7) | copy-start | bytes 1179652
  1.8 10.4 %copy-start.9 = (f32[256,128]{1,0:T(8,128)S(1)}, f32[256,128]{1,0:T(8,128)}, u32[]{:S(2)}) copy-start(f32[256,128]{1,0:T(8,128)} %param.9) | copy-start | bytes 393220
  3.0 9.3 %copy-start.10 = (f32[256,128]{1,0:T(8,128)S(1)}, f32[256,128]{1,0:T(8,128)}, u32[]{:S(2)}) copy-start(f32[256,128]{1,0:T(8,128)} %param.8) | copy-start | bytes 393220
  3.0 27.1 %all-to-all-start = ((f32[8,4,4,8,128]{4,3,1,2,0:T(8,128)}), f32[8,4,4,8,128]{4,3,1,2,0:T(8,128)S(1)}, u32[]{:S(2)}, u32[]{:S(2)}) async-start(f32[8,4,4,8,128]{4,3,1,2,0:T(8,128)} %copy.32), calls=%async_computation | async-start | bytes 1048576 | tf_op jit(solution)/shard_map/all_to_all | solution.py:35
  12.2 23.0 %copy-start.6 = (s32[256,128]{1,0:T(8,128)S(1)}, s32[256,128]{1,0:T(8,128)}, u32[]{:S(2)}) copy-start(s32[256,128]{1,0:T(8,128)} %param.10) | copy-start | bytes 393220
  30.9 12.8 %all-to-all-start.1 = ((f32[8,4,4,8,128]{4,3,0,2,1:T(8,128)}), f32[8,4,4,8,128]{4,3,0,2,1:T(8,128)S(1)}, u32[]{:S(2)}, u32[]{:S(2)}) async-start(f32[8,4,4,8,128]{4,3,0,2,1:T(8,128)} %copy.33), calls=%async_computation.1 | async-start | bytes 1048576 | tf_op jit(solution)/shard_map/all_to_all | solution.py:35
  43.8 0.8 copy-start.3
  48.1 6.8 %collective-permute-start = (f32[12,256,8]{1,2,0:T(8,128)S(1)}, f32[12,256,8]{1,2,0:T(8,128)S(1)}, u32[]{:S(2)}, u32[]{:S(2)}) collective-permute-start(f32[12,256,8]{1,2,0:T(8,128)S(1)} %copy.36), channel_id=1, source_target_pairs={{0,8},{8,16},{16,24},{24,32},{32,40},{40,48},{48,56},{56,64},{64,7... | collective-permute-start | bytes 294920 | tf_op jit(solution)/shard_map/ppermute | solution.py:51
  49.6 6.5 %collective-permute-start.1 = (f32[12,256,8]{1,2,0:T(8,128)}, f32[12,256,8]{1,2,0:T(8,128)}, u32[]{:S(2)}, u32[]{:S(2)}) collective-permute-start(f32[12,256,8]{1,2,0:T(8,128)} %copy.37), channel_id=1, source_target_pairs={{8,0},{16,8},{24,16},{32,24},{40,32},{48,40},{56,48},{64,56},{72,6... | collective-permute-start | bytes 294920 | tf_op jit(solution)/shard_map/ppermute | solution.py:53
  58.5 9.1 %copy-start.2 = (f32[12,256,8]{2,1,0:T(8,128)S(1)}, f32[12,256,8]{2,1,0:T(8,128)}, u32[]{:S(2)}) copy-start(f32[12,256,8]{2,1,0:T(8,128)} %copy.39) | copy-start | bytes 294916
  59.6 5.6 %collective-permute-start.2 = (f32[12,8,144]{2,1,0:T(8,128)S(1)}, f32[12,8,144]{2,1,0:T(8,128)S(1)}, u32[]{:S(2)}, u32[]{:S(2)}) collective-permute-start(f32[12,8,144]{2,1,0:T(8,128)S(1)} %get-tuple-element.33), channel_id=1, source_target_pairs={{0,1},{1,2},{2,3},{3,4},{4,5},{5,6},{6,7},{7,0},{8,9},{9,10},{10,1... | collective-permute-start | bytes 165896 | tf_op jit(solution)/shard_map/ppermute | solution.py:51
  63.6 4.0 %collective-permute-start.3 = (f32[12,8,144]{2,1,0:T(8,128)S(1)}, f32[12,8,144]{2,1,0:T(8,128)S(1)}, u32[]{:S(2)}, u32[]{:S(2)}) collective-permute-start(f32[12,8,144]{2,1,0:T(8,128)S(1)} %get-tuple-element.34), channel_id=1, source_target_pairs={{1,0},{2,1},{3,2},{4,3},{5,4},{6,5},{7,6},{0,7},{9,8},{10,9},{11,1... | collective-permute-start | bytes 165896 | tf_op jit(solution)/shard_map/ppermute | solution.py:53
  68.9 1.7 %copy-start = (f32[12,272,144]{2,1,0:T(8,128)}, f32[12,272,144]{2,1,0:T(8,128)S(1)}, u32[]{:S(2)}) copy-start(f32[12,272,144]{2,1,0:T(8,128)S(1)} %pad_maximum_fusion) | copy-start | bytes 5640196
  71.3 1.2 slice-start
  72.5 1.9 %copy-start.1 = (f32[12,272,144]{2,1,0:T(8,128)S(1)}, f32[12,272,144]{2,1,0:T(8,128)}, u32[]{:S(2)}) copy-start(f32[12,272,144]{2,1,0:T(8,128)} %copy-done) | copy-start | bytes 5640196
  83.5 1.0 copy-start.4
  85.1 9.5 %copy-start.5 = (f32[2,256,128]{2,1,0:T(8,128)}, f32[2,256,128]{2,1,0:T(8,128)S(1)}, u32[]{:S(2)}) copy-start(f32[2,256,128]{2,1,0:T(8,128)S(1)} %get-tuple-element.13) | copy-start | bytes 786436
  86.0 52.2 %all-to-all-start.2 = ((f32[2,256,128]{2,0,1:T(2,128)}), f32[2,256,128]{2,0,1:T(2,128)S(1)}, u32[]{:S(2)}, u32[]{:S(2)}) async-start(f32[2,256,128]{2,0,1:T(2,128)} %copy.41), calls=%async_computation.2 | async-start | bytes 524288 | tf_op jit(solution)/shard_map/all_to_all | solution.py:199
where the time goes:
time: 140 us; the launch traced here: 139 us
  blocking collectives  40.1 us (29%)
  waiting for transfers between devices  31.7 us (23%)
  starting transfers between devices  29.1 us (21%)
  local copies, waits for them, and re-layouts  19.5 us (14%)
  other arithmetic  17.7 us (13%)
    psum x4, blocking collectives, over_axes(): array = lax.psum(array, axis)  40.1 us
    all_to_all x2, waiting for transfers between devices, moved_by_axis(): filled = lax.all_to_all(filled, axes[k], k, k, tiled=True)  26.4 us
    all_to_all x2, starting transfers between devices, moved_by_axis(): filled = lax.all_to_all(filled, axes[k], k, k, tiled=True)  13.1 us
    all_to_all x1, starting transfers between devices, local(): lax.all_to_all(ice_stress, GX, split_axis=1, concat_axis=2, tiled=True)  7.11 us
    unnamed x27, local copies, waits for them, and re-layouts  5.2 us
    ppermute x2, starting transfers between devices, extended(): lax.ppermute(head, axis, [((i + 1) % count, i) for i in range(count)])  4.5 us
    ppermute x2, starting transfers between devices, extended(): lax.ppermute(tail, axis, [(i, (i + 1) % count) for i in range(count)])  4.3 us
    slice x2, local copies, waits for them, and re-layouts, extended(): lax.slice_in_dim(cells, cells.shape[dim] - width, cells.shape[dim], axis=...  3.52 us
  transfers between devices with their start and end apart: 7, of which 6 were waited for; matrix products, arithmetic and copies ran while one was open for 5% of the time, Pallas kernels for 0%

commit v1 on v0

v1 whole, which is shorter than its diff:
```python
import functools

import jax
import jax.numpy as jnp
from jax import lax
from jax.experimental import pallas as pl
from jax.experimental.pallas import tpu as pltpu
from jax.sharding import PartitionSpec as P

ITERS = 4
MESH = pl.DeviceIdType.MESH

U, V, A, B, C, Q, M, ICE = range(8)
TX, TY, OU, OV = range(4)


def lane_iota(rows=8):
    return lax.broadcasted_iota(jnp.int32, (rows, 128), 1)


def lanes_between(first, last, rows=8):
    lane = lane_iota(rows)
    return (lane >= first) & (lane < last)


def roll(x, shift):
    return pltpu.roll(x, shift % 128, 1) if shift % 128 else x


def placed(pieces):
    total = None
    for x, shift, first, last in pieces:
        moved = roll(x, shift)
        if total is None:
            total = jnp.where(lanes_between(first, last), moved, 0.0)
        else:
            total = jnp.where(lanes_between(first, last), moved, total)
    return total


def kernel(
    G, H,
    vel_ref, stress_ref, mass_ref, strength_ref, mask_ref, forcing_ref,
    vel_out, stress_out, res_out, ocean_out,
    X, F, BUV, MC, FV, RS, RP, RM, SP, RSP, PK, RK, VO, SO, IST, R1S, R1R, R2S, R2R,
    ld, fs, fr, ss, sr, las, lar, lon_s, lon_r, fls, flr, os_, or_, r1s, r1r, r2s, r2r, st,
):
    T = G
    S = T // 2 + 2
    R = 8 * T
    NY = H * R
    CH = min(8, T // 2)
    strip0 = T + 4
    gx = lax.axis_index("gx")
    gy = lax.axis_index("gy")
    east = lax.rem(gx + 1, G)
    west = lax.rem(gx + G - 1, G)
    north = gy + 1
    south = gy - 1
    has_north = gy < H - 1
    has_south = gy > 0

    def peer_x(k):
        return lax.rem(gx + k, G)

    def peer_y(k):
        return lax.rem(gy + k, H)

    bar = pltpu.get_barrier_semaphore()

    def greet_x(k, c):
        pl.semaphore_signal(bar, inc=1, device_id=(peer_x(k), gy), device_id_type=MESH)
        return c

    def greet_y(k, c):
        pl.semaphore_signal(bar, inc=1, device_id=(gx, peer_y(k)), device_id_type=MESH)
        return c

    lax.fori_loop(1, G, greet_x, 0)
    lax.fori_loop(1, H, greet_y, 0)

    own = pl.ds(16, R)
    loads = [
        pltpu.make_async_copy(forcing_ref, FV, ld.at[0]),
        pltpu.make_async_copy(vel_ref, X.at[pl.ds(0, 2), own, :], ld.at[1]),
        pltpu.make_async_copy(stress_ref, RS, ld.at[2]),
        pltpu.make_async_copy(mass_ref, X.at[M, own, :], ld.at[3]),
        pltpu.make_async_copy(strength_ref, RP, ld.at[4]),
        pltpu.make_async_copy(mask_ref, RM, ld.at[5]),
    ]
    for load in loads:
        load.start()

    for t in (0, T + 3, strip0 + S):
        X[:, 8 * t:8 * t + 8, :] = jnp.zeros((8, 8, 128), jnp.float32)

    @pl.when(jnp.logical_not(has_south))
    def _():
        X[:, 8:16, :] = jnp.zeros((8, 8, 128), jnp.float32)
        F[:, 8:16, :] = jnp.zeros((4, 8, 128), jnp.float32)
        RSP[0] = jnp.zeros((4, 128), jnp.float32)

    @pl.when(jnp.logical_not(has_north))
    def _():
        X[:, 8 * T + 16:8 * T + 24, :] = jnp.zeros((8, 8, 128), jnp.float32)
        F[:, 8 * T + 16:8 * T + 24, :] = jnp.zeros((4, 8, 128), jnp.float32)
        RSP[G + 1] = jnp.zeros((4, 128), jnp.float32)

    loads[0].wait()

    def columns(i):
        return pl.ds(pl.multiple_of(i * 128, 128), 128)

    def pack_forcing(i, c):
        before = columns(lax.rem(i + G - 1, G))
        after = columns(lax.rem(i + 1, G))
        pieces = []
        for f in range(4):
            pieces.append((FV[f, :, before], 16 * f + 8, 16 * f, 16 * f + 8))
            pieces.append((FV[f, :, after], 16 * f + 8, 16 * f + 8, 16 * f + 16))
        v = placed(pieces)
        SP[i] = jnp.where(lanes_between(0, 64, 4), v[0:4], roll(v, 64)[4:8])
        return c

    lax.fori_loop(0, G, pack_forcing, 0)
    own_band = pl.ds(pl.multiple_of(gx * 8 + 16, 8), 8)
    for f in range(4):
        F[f, own_band, :] = FV[f, :, columns(gx)]
    RSP[gx + 1] = SP[gx]

    for load in loads[1:]:
        load.wait()

    def derive(i, c):
        rows = pl.ds(pl.multiple_of(i * 8 * CH, 8), 8 * CH)
        wide = pl.ds(pl.multiple_of(i * 8 * CH + 16, 8), 8 * CH)
        ice = RM[rows, :].astype(jnp.float32)
        quarter = 0.25 * ice
        s0 = RS[0, rows, :]
        s1 = RS[1, rows, :]
        X[A, wide, :] = (s0 + s1) * quarter
        X[B, wide, :] = (s0 - s1) * quarter
        X[C, wide, :] = (RS[2, rows, :] * 0.5) * ice
        X[Q, wide, :] = (RP[rows, :] * 0.0625) * ice
        X[ICE, wide, :] = ice
        return c

    lax.fori_loop(0, T // CH, derive, 0)

    pl.semaphore_wait(bar, G - 1 + H - 1)

    def lat_copy(way):
        if way == 0:
            src, dst, to = 16, 8 * T + 16, south
        else:
            src, dst, to = 8 * T + 8, 8, north
        return pltpu.make_async_remote_copy(
            src_ref=X.at[:, pl.ds(src, 8), :], dst_ref=X.at[:, pl.ds(dst, 8), :],
            send_sem=las.at[way], recv_sem=lar.at[way], device_id=(gx, to), device_id_type=MESH)

    def forcing_copy(k):
        p = peer_x(k)
        return (
            pltpu.make_async_remote_copy(
                src_ref=FV.at[:, :, columns(p)], dst_ref=F.at[:, own_band, :],
                send_sem=fs.at[k], recv_sem=fr.at[gx], device_id=(p, gy), device_id_type=MESH),
            pltpu.make_async_remote_copy(
                src_ref=SP.at[p], dst_ref=RSP.at[gx + 1],
                send_sem=ss.at[k], recv_sem=sr.at[gx], device_id=(p, gy), device_id_type=MESH),
        )

    @pl.when(has_south)
    def _():
        lat_copy(0).start()

    @pl.when(has_north)
    def _():
        lat_copy(1).start()

    def send_forcing(k, c):
        for copy in forcing_copy(k):
            copy.start()
        return c

    lax.fori_loop(1, G, send_forcing, 0)

    @pl.when(has_south)
    def _():
        lat_copy(1).wait_recv()

    @pl.when(has_north)
    def _():
        lat_copy(0).wait_recv()

    def pack_columns(s, c):
        low = pl.ds(pl.multiple_of(s * 8 + 8, 8), 8)
        high = pl.ds(pl.multiple_of(s * 8 + 8 + R // 2, 8), 8)
        to_west, to_east = [], []
        for g, rows in ((0, low), (1, high)):
            for f in range(8):
                base = 64 * g + 8 * f
                x = X[f, rows, :]
                to_west.append((x, base, base, base + 8))
                to_east.append((x, base + 8, base, base + 8))
        here = pl.ds(pl.multiple_of(s * 8, 8), 8)
        PK[0, here, :] = placed(to_west)
        PK[1, here, :] = placed(to_east)
        return c

    lax.fori_loop(0, S, pack_columns, 0)

    def lon_copy(way):
        return pltpu.make_async_remote_copy(
            src_ref=PK.at[way], dst_ref=RK.at[way],
            send_sem=lon_s.at[way], recv_sem=lon_r.at[way],
            device_id=(west if way == 0 else east, gy), device_id_type=MESH)

    lon_copy(0).start()
    lon_copy(1).start()

    scale = 1.2 / NY
    band0 = gy * R

    def coriolis(first_row, half):
        row = first_row + lax.broadcasted_iota(jnp.int32, (8, 128), 0)
        if half:
            row = row + jnp.where(lane_iota() >= 48, half, 0)
        return 0.3 + 1.2 * (row.astype(jnp.float32) + 0.5) / NY

    def main_coriolis(t, c):
        rows = pl.ds(pl.multiple_of(t * 8 + 8, 8), 8)
        MC[rows, :] = X[M, rows, :] * coriolis(band0 + t * 8 - 8, 0)
        return c

    lax.fori_loop(0, T + 2, main_coriolis, 0)
    lon_copy(0).wait()
    lon_copy(1).wait()

    def strip_tile(own_low, own_high, from_west, west_shifts, from_east, east_shifts):
        pieces = []
        for g, x in ((0, own_low), (1, own_high)):
            at = 48 * g
            pieces.append((from_west, at - west_shifts[g], at, at + 8))
            pieces.append((x, at + 8, at + 8, at + 24))
            pieces.append((x, at + 24 - 112, at + 24, at + 40))
            pieces.append((from_east, at + 40 - east_shifts[g], at + 40, at + 48))
        return placed(pieces)

    def unpack_columns(s, c):
        low = pl.ds(pl.multiple_of(s * 8 + 8, 8), 8)
        high = pl.ds(pl.multiple_of(s * 8 + 8 + R // 2, 8), 8)
        here = pl.ds(pl.multiple_of(s * 8, 8), 8)
        there = pl.ds(pl.multiple_of(s * 8 + 8 * strip0, 8), 8)
        from_east = RK[0, here, :]
        from_west = RK[1, here, :]
        for f in range(8):
            shifts = (8 * f, 64 + 8 * f)
            x = strip_tile(X[f, low, :], X[f, high, :], from_west, shifts, from_east, shifts)
            X[f, there, :] = x
            if f == M:
                MC[there, :] = x * coriolis(band0 + s * 8 - 8, R // 2)
        return c

    lax.fori_loop(0, S, unpack_columns, 0)

    @pl.when(has_south)
    def _():
        lat_copy(0).wait_send()

    @pl.when(has_north)
    def _():
        lat_copy(1).wait_send()

    n_main = T // CH
    n_chunks = n_main + T // 2 // CH

    def chunk_row(c):
        return pl.multiple_of((2 + c * CH + jnp.where(c >= n_main, 3, 0)) * 8, 8)

    halo_rows = (8, 8 * (T + 2), 8 * strip0, 8 * (strip0 + S - 1))

    def relax_stress(row, count):
        rows = pl.ds(row, count)
        up = pl.ds(row + 1, count)
        down = pl.ds(row - 1, count)
        u = X[U, rows, :]
        v = X[V, rows, :]
        east_dx = roll(u, -1) - roll(u, 1)
        north_dx = roll(v, -1) - roll(v, 1)
        east_dy = X[U, up, :] - X[U, down, :]
        north_dy = X[V, up, :] - X[V, down, :]
        tension = east_dx - north_dy
        shear = east_dy + north_dx
        g = 2.0 * (east_dx + north_dy)
        h = 0.5 * tension
        inverse = lax.rsqrt(g * g + (tension * tension + shear * shear) + 0.04)
        q = X[Q, rows, :]
        qr = q * inverse
        X[A, rows, :] = 0.75 * X[A, rows, :] + ((g + h) * qr - q)
        X[B, rows, :] = 0.75 * X[B, rows, :] + ((g - h) * qr - q)
        X[C, rows, :] = 0.75 * X[C, rows, :] + (0.5 * shear) * qr

    def drag_of(u, v, ou, ov):
        du = ou - u
        dv = ov - v
        return jnp.sqrt(du * du + dv * dv + 0.01)

    def new_velocity(row, count, first):
        rows = pl.ds(row, count)
        up = pl.ds(row + 1, count)
        down = pl.ds(row - 1, count)
        a = X[A, rows, :]
        c = X[C, rows, :]
        force_east = (roll(a, -1) - roll(a, 1)) + (X[C, up, :] - X[C, down, :])
        force_north = (roll(c, -1) - roll(c, 1)) + (X[B, up, :] - X[B, down, :])
        u = X[U, rows, :]
        v = X[V, rows, :]
        ou = F[OU, rows, :]
        ov = F[OV, rows, :]
        m = X[M, rows, :]
        mc = MC[rows, :]
        if first:
            bu = m * u + F[TX, rows, :]
            bv = m * v + F[TY, rows, :]
            BUV[0, rows, :] = bu
            BUV[1, rows, :] = bv
        else:
            bu = BUV[0, rows, :]
            bv = BUV[1, rows, :]
        drag = drag_of(u, v, ou, ov)
        m4 = 4.0 * m
        w = X[ICE, rows, :] / (m4 + m + drag)
        new_u = (m4 * u + mc * v + (bu + force_east + drag * ou)) * w
        new_v = (m4 * v - mc * u + (bv + force_north + drag * ov)) * w
        du = new_u - u
        dv = new_v - v
        change = du * du + dv * dv
        total = change[0:8]
        for t in range(1, count // 8):
            total = total + change[8 * t:8 * t + 8]
        return new_u, new_v, total

    main_lanes = lanes_between(8, 120)
    strip_lanes = (
        lanes_between(8, 16) | lanes_between(32, 40) | lanes_between(56, 64) | lanes_between(80, 88))
    zero = jnp.zeros((8, 128), jnp.float32)

    def stress_sweep():
        def body(c, carry):
            relax_stress(chunk_row(c), 8 * CH)
            return carry

        lax.fori_loop(0, n_chunks, body, 0)
        for row in halo_rows:
            relax_stress(row, 8)

    def velocity_sweep(first):
        def body(c, acc):
            row = chunk_row(c)
            new_u, new_v, total = new_velocity(row, 8 * CH, first)
            X[U, pl.ds(row, 8 * CH), :] = new_u
            X[V, pl.ds(row, 8 * CH), :] = new_v
            is_main = jnp.where(c < n_main, 1.0, 0.0)
            weight = jnp.where(main_lanes, is_main, 0.0) + jnp.where(strip_lanes, 1.0 - is_main, 0.0)
            return acc + total * weight

        acc = lax.fori_loop(0, n_chunks, body, zero)
        for row in halo_rows:
            new_u, new_v, _ = new_velocity(row, 8, first)
            X[U, pl.ds(row, 8), :] = new_u
            X[V, pl.ds(row, 8), :] = new_v
        return acc

    stress_sweep()

    def wait_band(s):
        band = pl.ds(pl.multiple_of(s * 8 + 16, 8), 8)
        pltpu.make_async_remote_copy(
            src_ref=FV.at[:, :, columns(0)], dst_ref=F.at[:, band, :],
            send_sem=fs.at[0], recv_sem=fr.at[s], device_id=(east, gy), device_id_type=MESH).wait_recv()
        pltpu.make_async_remote_copy(
            src_ref=SP.at[0], dst_ref=RSP.at[s + 1],
            send_sem=ss.at[0], recv_sem=sr.at[s], device_id=(east, gy), device_id_type=MESH).wait_recv()

    def edge_copy(way):
        if way == 0:
            src, dst, one, other, to = 16, 8 * T + 16, 1, G + 1, south
        else:
            src, dst, one, other, to = 8 * T + 8, 8, G, 0, north
        return (
            pltpu.make_async_remote_copy(
                src_ref=F.at[:, pl.ds(src, 8), :], dst_ref=F.at[:, pl.ds(dst, 8), :],
                send_sem=fls.at[2 * way], recv_sem=flr.at[2 * way],
                device_id=(gx, to), device_id_type=MESH),
            pltpu.make_async_remote_copy(
                src_ref=RSP.at[one], dst_ref=RSP.at[other],
                send_sem=fls.at[2 * way + 1], recv_sem=flr.at[2 * way + 1],
                device_id=(gx, to), device_id_type=MESH),
        )

    @pl.when(gx != 0)
    def _():
        wait_band(0)

    @pl.when(has_south)
    def _():
        for copy in edge_copy(0):
            copy.start()

    @pl.when(gx != G - 1)
    def _():
        wait_band(G - 1)

    @pl.when(has_north)
    def _():
        for copy in edge_copy(1):
            copy.start()

    def wait_other(s, c):
        @pl.when(s != gx)
        def _():
            wait_band(s)

        return c

    lax.fori_loop(1, G - 1, wait_other, 0)

    @pl.when(has_south)
    def _():
        for copy in edge_copy(1):
            copy.wait_recv()

    @pl.when(has_north)
    def _():
        for copy in edge_copy(0):
            copy.wait_recv()

    def unpack_forcing(s, c):
        low = pl.ds(pl.multiple_of(s * 8 + 8, 8), 8)
        high = pl.ds(pl.multiple_of(s * 8 + 8 + R // 2, 8), 8)
        there = pl.ds(pl.multiple_of(s * 8 + 8 * strip0, 8), 8)
        halves = []
        for part in (RSP[s], RSP[s + G // 2]):
            halves.append(jnp.concatenate([part, roll(part, 64)], axis=0))
        for f in range(4):
            pieces = []
            for g, rows in ((0, low), (1, high)):
                at = 48 * g
                x = F[f, rows, :]
                pieces.append((halves[g], at - 16 * f, at, at + 8))
                pieces.append((x, at + 8, at + 8, at + 24))
                pieces.append((x, at + 24 - 112, at + 24, at + 40))
                pieces.append((halves[g], at + 40 - 16 * f - 8, at + 40, at + 48))
            F[f, there, :] = placed(pieces)
        return c

    lax.fori_loop(0, S, unpack_forcing, 0)

    sums = [velocity_sweep(True)]
    stress_sweep()
    sums.append(velocity_sweep(False))
    stress_sweep()
    sums.append(velocity_sweep(False))
    stress_sweep()

    def last_strip(c, acc):
        row = chunk_row(c)
        new_u, new_v, total = new_velocity(row, 8 * CH, False)
        X[U, pl.ds(row, 8 * CH), :] = new_u
        X[V, pl.ds(row, 8 * CH), :] = new_v
        return acc + total

    strip_sum = lax.fori_loop(n_main, n_chunks, last_strip, zero)
    rows_last = 8 * CH
    left = lanes_between(0, 8, rows_last)
    right = lanes_between(120, 128, rows_last)

    def merged(x, f, strip_rows, g):
        strip = X[f, strip_rows, :]
        x = jnp.where(left, roll(strip, -(48 * g + 8)), x)
        return jnp.where(right, roll(strip, 88 - 48 * g), x)

    def last_main(g, c, acc):
        first = pl.multiple_of(c * 8 * CH + g * R // 2, 8)
        row = pl.multiple_of(first + 16, 8)
        rows = pl.ds(row, rows_last)
        out = pl.ds(first, rows_last)
        strip_rows = pl.ds(pl.multiple_of((strip0 + 1) * 8 + c * 8 * CH, 8), rows_last)
        new_u, new_v, total = new_velocity(row, rows_last, False)
        new_u = merged(new_u, U, strip_rows, g)
        new_v = merged(new_v, V, strip_rows, g)
        VO[0, out, :] = new_u
        VO[1, out, :] = new_v
        a = merged(X[A, rows, :], A, strip_rows, g)
        b = merged(X[B, rows, :], B, strip_rows, g)
        SO[0, out, :] = 2.0 * (a + b)
        SO[1, out, :] = 2.0 * (a - b)
        SO[2, out, :] = 2.0 * merged(X[C, rows, :], C, strip_rows, g)
        ou = F[OU, rows, :]
        ov = F[OV, rows, :]
        drag = drag_of(new_u, new_v, ou, ov) * X[ICE, rows, :]
        east_stress = drag * (new_u - ou)
        north_stress = drag * (new_v - ov)
        for t in range(CH):
            band = c * CH + g * (T // 2) + t
            IST[band, 0] = east_stress[8 * t:8 * t + 8]
            IST[band, 1] = north_stress[8 * t:8 * t + 8]
        return acc + total

    main_sum = zero
    for g in range(2):
        main_sum = lax.fori_loop(0, T // 2 // CH, functools.partial(last_main, g), main_sum)
    sums.append(jnp.where(main_lanes, main_sum, 0.0) + jnp.where(strip_lanes, strip_sum, 0.0))

    def out_copy(k):
        p = peer_x(k)
        return pltpu.make_async_remote_copy(
            src_ref=IST.at[p], dst_ref=ocean_out.at[:, :, columns(gx)],
            send_sem=os_.at[k], recv_sem=or_.at[gx], device_id=(p, gy), device_id_type=MESH)

    def send_out(k, c):
        out_copy(k).start()
        return c

    lax.fori_loop(1, G, send_out, 0)

    lane = lane_iota(1)
    row = jnp.zeros((1, 128), jnp.float32)
    for k, acc in enumerate(sums):
        total = jnp.sum(jnp.sum(acc, axis=0, keepdims=True), axis=1, keepdims=True)
        row = jnp.where(lane == k, total, row)
    R1S[...] = row
    R1R[gx] = row

    def sum_copy_x(k):
        return pltpu.make_async_remote_copy(
            src_ref=R1S, dst_ref=R1R.at[gx],
            send_sem=r1s.at[k], recv_sem=r1r.at[gx], device_id=(peer_x(k), gy), device_id_type=MESH)

    def sum_copy_y(k):
        return pltpu.make_async_remote_copy(
            src_ref=R2S, dst_ref=R2R.at[gy],
            send_sem=r2s.at[k], recv_sem=r2r.at[gy], device_id=(gx, peer_y(k)), device_id_type=MESH)

    def send_x(k, c):
        sum_copy_x(k).start()
        return c

    lax.fori_loop(1, G, send_x, 0)

    stores = [
        pltpu.make_async_copy(VO, vel_out, st.at[0]),
        pltpu.make_async_copy(SO, stress_out, st.at[1]),
        pltpu.make_async_copy(IST.at[gx], ocean_out.at[:, :, columns(gx)], st.at[2]),
    ]
    for store in stores:
        store.start()

    def wait_sum_x(k, c):
        s = peer_x(k)
        pltpu.make_async_remote_copy(
            src_ref=R1S, dst_ref=R1R.at[s], send_sem=r1s.at[k], recv_sem=r1r.at[s],
            device_id=(s, gy), device_id_type=MESH).wait()
        return c

    lax.fori_loop(1, G, wait_sum_x, 0)
    over_x = jnp.sum(R1R[...], axis=0)
    R2S[...] = over_x
    R2R[gy] = over_x

    def send_y(k, c):
        sum_copy_y(k).start()
        return c

    lax.fori_loop(1, H, send_y, 0)

    def wait_sum_y(k, c):
        s = peer_y(k)
        pltpu.make_async_remote_copy(
            src_ref=R2S, dst_ref=R2R.at[s], send_sem=r2s.at[k], recv_sem=r2r.at[s],
            device_id=(gx, s), device_id_type=MESH).wait()
        return c

    lax.fori_loop(1, H, wait_sum_y, 0)
    over_all = jnp.sum(R2R[...], axis=0)
    for k in range(ITERS):
        res_out[k] = over_all[0, k]

    def end_forcing(k, c):
        for copy in forcing_copy(k):
            copy.wait_send()
        return c

    lax.fori_loop(1, G, end_forcing, 0)

    @pl.when(has_south)
    def _():
        for copy in edge_copy(0):
            copy.wait_send()

    @pl.when(has_north)
    def _():
        for copy in edge_copy(1):
            copy.wait_send()

    def end_out(k, c):
        s = peer_x(k)
        pltpu.make_async_remote_copy(
            src_ref=IST.at[s], dst_ref=ocean_out.at[:, :, columns(s)],
            send_sem=os_.at[k], recv_sem=or_.at[s], device_id=(s, gy), device_id_type=MESH).wait()
        return c

    lax.fori_loop(1, G, end_out, 0)
    for store in stores:
        store.wait()


def local(G, H, velocity, stress, ice_mass, strength, land_mask, ocean_forcing):
    T = G
    S = T // 2 + 2
    R = 8 * T
    rows = 8 * (T + 5 + S)
    f32 = jnp.float32
    anywhere = pl.BlockSpec(memory_space=pl.ANY)
    dma = pltpu.SemaphoreType.DMA
    return pl.pallas_call(
        functools.partial(kernel, G, H),
        out_shape=(
            jax.ShapeDtypeStruct((2, R, 128), f32),
            jax.ShapeDtypeStruct((3, R, 128), f32),
            jax.ShapeDtypeStruct((ITERS,), f32),
            jax.ShapeDtypeStruct((2, 8, 128 * G), f32),
        ),
        in_specs=[anywhere] * 6,
        out_specs=(anywhere, anywhere, pl.BlockSpec(memory_space=pltpu.SMEM), anywhere),
        scratch_shapes=[
            pltpu.VMEM((8, rows, 128), f32),
            pltpu.VMEM((4, rows, 128), f32),
            pltpu.VMEM((2, rows, 128), f32),
            pltpu.VMEM((rows, 128), f32),
            pltpu.VMEM((4, 8, 128 * G), f32),
            pltpu.VMEM((3, R, 128), f32),
            pltpu.VMEM((R, 128), f32),
            pltpu.VMEM((R, 128), jnp.int32),
            pltpu.VMEM((G, 4, 128), f32),
            pltpu.VMEM((G + 2, 4, 128), f32),
            pltpu.VMEM((2, 8 * S, 128), f32),
            pltpu.VMEM((2, 8 * S, 128), f32),
            pltpu.VMEM((2, R, 128), f32),
            pltpu.VMEM((3, R, 128), f32),
            pltpu.VMEM((G, 2, 8, 128), f32),
            pltpu.VMEM((1, 128), f32),
            pltpu.VMEM((G, 1, 128), f32),
            pltpu.VMEM((1, 128), f32),
            pltpu.VMEM((H, 1, 128), f32),
            dma((6,)), dma((G,)), dma((G,)), dma((G,)), dma((G,)),
            dma((2,)), dma((2,)), dma((2,)), dma((2,)), dma((4,)), dma((4,)),
            dma((G,)), dma((G,)), dma((G,)), dma((G,)), dma((H,)), dma((H,)), dma((3,)),
        ],
        compiler_params=pltpu.CompilerParams(collective_id=0, has_side_effects=True),
    )(velocity, stress, ice_mass, strength, land_mask, ocean_forcing)


def solution(mesh):
    block = P(None, "gy", "gx")
    plane = P("gy", "gx")
    bands = P(None, ("gy", "gx"), None)
    return jax.shard_map(
        functools.partial(local, mesh.shape["gx"], mesh.shape["gy"]),
        mesh=mesh,
        in_specs=(block, block, plane, plane, plane, bands),
        out_specs=(block, block, P(), bands),
        check_vma=False,
    )
```

time: 140 us -> 66 us (0.47)
  Pallas kernels: 0 us -> 61.5 us
  blocking collectives: 40.1 us -> 0 us
  waiting for transfers between devices: 31.7 us -> 0 us
  starting transfers between devices: 29.1 us -> 0 us
  other arithmetic: 17.7 us -> 0 us
  local copies, waits for them, and re-layouts: 19.5 us -> 3.69 us
    pallas_call x0 -> x1, Pallas kernels: none -> 61.5 us  [local(): pl.pallas_call(functools.partial(kernel, G, H), out_shape=(jax.ShapeDtype...]
    psum x4 -> x0, blocking collectives: 40.1 us -> none  [over_axes(): array = lax.psum(array, axis)]
    all_to_all x3 -> x0, waiting for transfers between devices: 26.4 us -> none  [the longest x2 26.4 us: moved_by_axis(): filled = lax.all_to_all(filled, axes[k], k, k, tiled=True)]
    all_to_all x3 -> x0, starting transfers between devices: 20.3 us -> none  [the longest x2 13.1 us: moved_by_axis(): filled = lax.all_to_all(filled, axes[k], k, k, tiled=True)]
    ppermute x4 -> x0, starting transfers between devices: 8.8 us -> none  [the longest x2 4.5 us: extended(): lax.ppermute(head, axis, [((i + 1) % count, i) for i in range(count)])]
    slice x16 -> x0, local copies, waits for them, and re-layouts: 7.56 us -> none  [the longest x2 3.52 us: extended(): lax.slice_in_dim(cells, cells.shape[dim] - width, cells.shape[dim], axis=...]
    mul x17 -> x0, other arithmetic: 7.4 us -> none  [the longest x3 2.93 us: relax_velocity(): (BETA * vel[1] + vel_start[1] + (force_north + forcing[1] + drag_rate * f...]
    another operation x9 -> x0, other arithmetic: 6.1 us -> none  [the longest x8 3.42 us: relax_stress(): jnp.stack([strength * (divergence / delta_rate - 1.0), strength * tension...]
  transfers between devices with their start and end apart: 7 -> 0, of which waited for: 6 -> 0; matrix products, arithmetic and copies ran while one was open for 5% -> 0% of each run, Pallas kernels for 0% -> 0%
where the time goes in v1:
time: 66 us; the launch traced here: 65.9 us
  Pallas kernels  61.5 us (93%)
  local copies, waits for them, and re-layouts  3.69 us (6%)
    pallas_call x1, Pallas kernels, local(): pl.pallas_call(functools.partial(kernel, G, H), out_shape=(jax.ShapeDtype...  61.5 us
    unnamed x10, local copies, waits for them, and re-layouts  3.69 us

profile of v1, /device:TPU:1, one launch (start us, length us, event | category | flops | bytes accessed | tf_op | source)
XLA Modules:
  0.0 65.9 jit_solution(12650192291039453746)
XLA Ops:
  0.6 61.5 %shard_map.93 = (f32[2,256,128]{2,1,0:T(8,128)}, f32[3,256,128]{2,1,0:T(8,128)}, f32[4]{0:T(128)}, f32[2,8,4096]{2,1,0:T(8,128)}) custom-call(f32[2,256,128]{2,1,0:T(8,128)} %vel_ref.1, f32[3,256,128]{2,1,0:T(8,128)} %stress_ref.1, f32[256,128]{1,0:T(8,128)} %mass_ref.1, f32[256,128]{1,0:T(8,128)} %strength_ref.1, s32[256,128]{1,0:T(8,128)} %mask_ref.1, ...), custom_call_target="tpu_custom_call" | custom-call | tf_op jit(solution)/shard_map/pallas_call | solution.py:626
  62.2 0.0 copy-start
  62.2 1.7 %copy.14 = f32[2,256,128]{2,1,0:T(8,128)} copy(f32[2,256,128]{2,1,0:T(8,128)} %get-tuple-element.8) | data formatting | bytes 524288
  63.9 0.0 copy-done
  63.9 0.0 copy-start.2
  63.9 0.0 copy-start.1
  63.9 0.7 %copy.15 = f32[3,256,128]{2,1,0:T(8,128)} copy(f32[3,256,128]{2,1,0:T(8,128)S(1)} %copy-done) | data formatting | bytes 786432
  64.7 0.0 copy-done.2
  64.7 0.5 copy.16
  65.2 0.0 copy-done.1
  65.2 0.7 %copy.17 = f32[2,8,4096]{2,1,0:T(8,128)} copy(f32[2,8,4096]{2,1,0:T(8,128)S(1)} %copy-done.1) | data formatting | bytes 524288
Async XLA Ops:
  62.2 1.7 %copy-start = (f32[3,256,128]{2,1,0:T(8,128)S(1)}, f32[3,256,128]{2,1,0:T(8,128)}, u32[]{:S(2)}) copy-start(f32[3,256,128]{2,1,0:T(8,128)} %get-tuple-element.9) | copy-start | bytes 1179652
  63.9 0.8 %copy-start.2 = (f32[4]{0:T(128)S(1)}, f32[4]{0:T(128)}, u32[]{:S(2)}) copy-start(f32[4]{0:T(128)} %get-tuple-element.10) | copy-start | bytes 52
  63.9 1.3 %copy-start.1 = (f32[2,8,4096]{2,1,0:T(8,128)S(1)}, f32[2,8,4096]{2,1,0:T(8,128)}, u32[]{:S(2)}) copy-start(f32[2,8,4096]{2,1,0:T(8,128)} %get-tuple-element.11) | copy-start | bytes 786436

commit v2 on v1

--- a/solution.py
+++ b/solution.py
@@ -28,13 +28,9 @@
 
 
 def placed(pieces):
-    total = None
+    total = 0.0
     for x, shift, first, last in pieces:
-        moved = roll(x, shift)
-        if total is None:
-            total = jnp.where(lanes_between(first, last), moved, 0.0)
-        else:
-            total = jnp.where(lanes_between(first, last), moved, total)
+        total = jnp.where(lanes_between(first, last, x.shape[0]), roll(x, shift), total)
     return total
 
 
@@ -42,14 +38,16 @@
     G, H,
     vel_ref, stress_ref, mass_ref, strength_ref, mask_ref, forcing_ref,
     vel_out, stress_out, res_out, ocean_out,
-    X, F, BUV, MC, FV, RS, RP, RM, SP, RSP, PK, RK, VO, SO, IST, R1S, R1R, R2S, R2R,
-    ld, fs, fr, ss, sr, las, lar, lon_s, lon_r, fls, flr, os_, or_, r1s, r1r, r2s, r2r, st,
+    X, F, BUV, MC, FV, RS, RP, RM, SP, RSP, PK, RK, CS, CR, IST, R1S, R1R, R2S, R2R,
+    ld, fs, fr, ss, sr, las, lar, lon_s, lon_r, cs, cr, fls, flr, os_, or_, r1s, r1r, r2s, r2r, st,
 ):
     T = G
     S = T // 2 + 2
     R = 8 * T
     NY = H * R
     CH = min(8, T // 2)
+    PU = min(8, T // 2)
+    SU = min(9, S)
     strip0 = T + 4
     gx = lax.axis_index("gx")
     gy = lax.axis_index("gy")
@@ -78,6 +76,16 @@
 
     lax.fori_loop(1, G, greet_x, 0)
     lax.fori_loop(1, H, greet_y, 0)
+
+    @pl.when(has_south)
+    def _():
+        for to in (west, east):
+            pl.semaphore_signal(bar, inc=1, device_id=(to, south), device_id_type=MESH)
+
+    @pl.when(has_north)
+    def _():
+        for to in (west, east):
+            pl.semaphore_signal(bar, inc=1, device_id=(to, north), device_id_type=MESH)
 
     own = pl.ds(16, R)
     loads = [
@@ -99,30 +107,34 @@
         X[:, 8:16, :] = jnp.zeros((8, 8, 128), jnp.float32)
         F[:, 8:16, :] = jnp.zeros((4, 8, 128), jnp.float32)
         RSP[0] = jnp.zeros((4, 128), jnp.float32)
+        CR[0:2] = jnp.zeros((2, 8, 128), jnp.float32)
 
     @pl.when(jnp.logical_not(has_north))
     def _():
         X[:, 8 * T + 16:8 * T + 24, :] = jnp.zeros((8, 8, 128), jnp.float32)
         F[:, 8 * T + 16:8 * T + 24, :] = jnp.zeros((4, 8, 128), jnp.float32)
         RSP[G + 1] = jnp.zeros((4, 128), jnp.float32)
+        CR[2:4] = jnp.zeros((2, 8, 128), jnp.float32)
 
     loads[0].wait()
 
     def columns(i):
         return pl.ds(pl.multiple_of(i * 128, 128), 128)
 
-    def pack_forcing(i, c):
-        before = columns(lax.rem(i + G - 1, G))
-        after = columns(lax.rem(i + 1, G))
-        pieces = []
-        for f in range(4):
-            pieces.append((FV[f, :, before], 16 * f + 8, 16 * f, 16 * f + 8))
-            pieces.append((FV[f, :, after], 16 * f + 8, 16 * f + 8, 16 * f + 16))
-        v = placed(pieces)
-        SP[i] = jnp.where(lanes_between(0, 64, 4), v[0:4], roll(v, 64)[4:8])
-        return c
-
-    lax.fori_loop(0, G, pack_forcing, 0)
+    def pack_forcing(group, c):
+        for t in range(CH):
+            i = group * CH + t
+            before = columns(lax.rem(i + G - 1, G))
+            after = columns(lax.rem(i + 1, G))
+            pieces = []
+            for f in range(4):
+                pieces.append((FV[f, :, before], 16 * f + 8, 16 * f, 16 * f + 8))
+                pieces.append((FV[f, :, after], 16 * f + 8, 16 * f + 8, 16 * f + 16))
+            v = placed(pieces)
+            SP[i] = jnp.where(lanes_between(0, 64, 4), v[0:4], roll(v, 64)[4:8])
+        return c
+
+    lax.fori_loop(0, G // CH, pack_forcing, 0)
     own_band = pl.ds(pl.multiple_of(gx * 8 + 16, 8), 8)
     for f in range(4):
         F[f, own_band, :] = FV[f, :, columns(gx)]
@@ -147,7 +159,32 @@
 
     lax.fori_loop(0, T // CH, derive, 0)
 
-    pl.semaphore_wait(bar, G - 1 + H - 1)
+    def edge_columns(groups):
+        to_west, to_east = [], []
+        for g, rows in groups:
+            for f in range(8):
+                base = 64 * g + 8 * f
+                x = X[f, rows, :]
+                to_west.append((x, base, base, base + 8))
+                to_east.append((x, base + 8, base, base + 8))
+        return placed(to_west), placed(to_east)
+
+    def pack_columns(c, carry):
+        low = pl.ds(pl.multiple_of(c * 8 * PU + 16, 8), 8 * PU)
+        high = pl.ds(pl.multiple_of(c * 8 * PU + 16 + R // 2, 8), 8 * PU)
+        here = pl.ds(pl.multiple_of(c * 8 * PU + 8, 8), 8 * PU)
+        PK[0, here, :], PK[1, here, :] = edge_columns(((0, low), (1, high)))
+        return carry
+
+    lax.fori_loop(0, T // 2 // PU, pack_columns, 0)
+    first, last = pl.ds(0, 8), pl.ds(8 * S - 8, 8)
+    PK[0, first, :], PK[1, first, :] = edge_columns(((1, pl.ds(8 + R // 2, 8)),))
+    PK[0, last, :], PK[1, last, :] = edge_columns(((0, pl.ds(16 + R // 2, 8)),))
+    CS[0], CS[1] = edge_columns(((0, pl.ds(8 * T + 8, 8)),))
+    CS[2], CS[3] = edge_columns(((1, pl.ds(16, 8)),))
+
+    diagonal = 2 * has_south.astype(jnp.int32) + 2 * has_north.astype(jnp.int32)
+    pl.semaphore_wait(bar, G - 1 + H - 1 + diagonal)
 
     def lat_copy(way):
         if way == 0:
@@ -157,6 +194,17 @@
         return pltpu.make_async_remote_copy(
             src_ref=X.at[:, pl.ds(src, 8), :], dst_ref=X.at[:, pl.ds(dst, 8), :],
             send_sem=las.at[way], recv_sem=lar.at[way], device_id=(gx, to), device_id_type=MESH)
+
+    def corner_copy(n):
+        return pltpu.make_async_remote_copy(
+            src_ref=CS.at[n], dst_ref=CR.at[n], send_sem=cs.at[n], recv_sem=cr.at[n],
+            device_id=(east if n % 2 else west, north if n < 2 else south), device_id_type=MESH)
+
+    def lon_copy(way):
+        return pltpu.make_async_remote_copy(
+            src_ref=PK.at[way], dst_ref=RK.at[way],
+            send_sem=lon_s.at[way], recv_sem=lon_r.at[way],
+            device_id=(west if way == 0 else east, gy), device_id_type=MESH)
 
     def forcing_copy(k):
         p = peer_x(k)
@@ -169,13 +217,20 @@
                 send_sem=ss.at[k], recv_sem=sr.at[gx], device_id=(p, gy), device_id_type=MESH),
         )
 
+    lon_copy(0).start()
+    lon_copy(1).start()
+
     @pl.when(has_south)
     def _():
         lat_copy(0).start()
+        corner_copy(2).start()
+        corner_copy(3).start()
 
     @pl.when(has_north)
     def _():
         lat_copy(1).start()
+        corner_copy(0).start()
+        corner_copy(1).start()
 
     def send_forcing(k, c):
         for copy in forcing_copy(k):
@@ -187,54 +242,34 @@
     @pl.when(has_south)
     def _():
         lat_copy(1).wait_recv()
+        corner_copy(0).wait_recv()
+        corner_copy(1).wait_recv()
 
     @pl.when(has_north)
     def _():
         lat_copy(0).wait_recv()
-
-    def pack_columns(s, c):
-        low = pl.ds(pl.multiple_of(s * 8 + 8, 8), 8)
-        high = pl.ds(pl.multiple_of(s * 8 + 8 + R // 2, 8), 8)
-        to_west, to_east = [], []
-        for g, rows in ((0, low), (1, high)):
-            for f in range(8):
-                base = 64 * g + 8 * f
-                x = X[f, rows, :]
-                to_west.append((x, base, base, base + 8))
-                to_east.append((x, base + 8, base, base + 8))
-        here = pl.ds(pl.multiple_of(s * 8, 8), 8)
-        PK[0, here, :] = placed(to_west)
-        PK[1, here, :] = placed(to_east)
-        return c
-
-    lax.fori_loop(0, S, pack_columns, 0)
-
-    def lon_copy(way):
-        return pltpu.make_async_remote_copy(
-            src_ref=PK.at[way], dst_ref=RK.at[way],
-            send_sem=lon_s.at[way], recv_sem=lon_r.at[way],
-            device_id=(west if way == 0 else east, gy), device_id_type=MESH)
-
-    lon_copy(0).start()
-    lon_copy(1).start()
-
-    scale = 1.2 / NY
+        corner_copy(2).wait_recv()
+        corner_copy(3).wait_recv()
+
     band0 = gy * R
 
-    def coriolis(first_row, half):
-        row = first_row + lax.broadcasted_iota(jnp.int32, (8, 128), 0)
+    def coriolis(first_row, half, count):
+        row = first_row + lax.broadcasted_iota(jnp.int32, (count, 128), 0)
         if half:
-            row = row + jnp.where(lane_iota() >= 48, half, 0)
+            row = row + jnp.where(lane_iota(count) >= 48, half, 0)
         return 0.3 + 1.2 * (row.astype(jnp.float32) + 0.5) / NY
 
     def main_coriolis(t, c):
-        rows = pl.ds(pl.multiple_of(t * 8 + 8, 8), 8)
-        MC[rows, :] = X[M, rows, :] * coriolis(band0 + t * 8 - 8, 0)
-        return c
-
-    lax.fori_loop(0, T + 2, main_coriolis, 0)
-    lon_copy(0).wait()
-    lon_copy(1).wait()
+        rows = pl.ds(pl.multiple_of(t * 16 + 8, 8), 16)
+        MC[rows, :] = X[M, rows, :] * coriolis(band0 + t * 16 - 8, 0, 16)
+        return c
+
+    lax.fori_loop(0, T // 2 + 1, main_coriolis, 0)
+    for way in range(2):
+        lon_copy(way).wait()
+        RK[way, 0:8, :] = jnp.where(lanes_between(0, 64), CR[way], RK[way, 0:8, :])
+        RK[way, 8 * S - 8:8 * S, :] = jnp.where(
+            lanes_between(64, 128), CR[way + 2], RK[way, 8 * S - 8:8 * S, :])
 
     def strip_tile(own_low, own_high, from_west, west_shifts, from_east, east_shifts):
         pieces = []
@@ -246,11 +281,15 @@
             pieces.append((from_east, at + 40 - east_shifts[g], at + 40, at + 48))
         return placed(pieces)
 
-    def unpack_columns(s, c):
-        low = pl.ds(pl.multiple_of(s * 8 + 8, 8), 8)
-        high = pl.ds(pl.multiple_of(s * 8 + 8 + R // 2, 8), 8)
-        here = pl.ds(pl.multiple_of(s * 8, 8), 8)
-        there = pl.ds(pl.multiple_of(s * 8 + 8 * strip0, 8), 8)
+    def strip_places(c):
+        low = pl.ds(pl.multiple_of(c * 8 * SU + 8, 8), 8 * SU)
+        high = pl.ds(pl.multiple_of(c * 8 * SU + 8 + R // 2, 8), 8 * SU)
+        there = pl.ds(pl.multiple_of(c * 8 * SU + 8 * strip0, 8), 8 * SU)
+        return low, high, there
+
+    def unpack_columns(c, carry):
+        low, high, there = strip_places(c)
+        here = pl.ds(pl.multiple_of(c * 8 * SU, 8), 8 * SU)
         from_east = RK[0, here, :]
         from_west = RK[1, here, :]
         for f in range(8):
@@ -258,18 +297,22 @@
             x = strip_tile(X[f, low, :], X[f, high, :], from_west, shifts, from_east, shifts)
             X[f, there, :] = x
             if f == M:
-                MC[there, :] = x * coriolis(band0 + s * 8 - 8, R // 2)
-        return c
-
-    lax.fori_loop(0, S, unpack_columns, 0)
+                MC[there, :] = x * coriolis(band0 + c * 8 * SU - 8, R // 2, 8 * SU)
+        return carry
+
+    lax.fori_loop(0, S // SU, unpack_columns, 0)
 
     @pl.when(has_south)
     def _():
         lat_copy(0).wait_send()
+        corner_copy(2).wait_send()
+        corner_copy(3).wait_send()
 
     @pl.when(has_north)
     def _():
         lat_copy(1).wait_send()
+        corner_copy(0).wait_send()
+        corner_copy(1).wait_send()
 
     n_main = T // CH
     n_chunks = n_main + T // 2 // CH
@@ -435,26 +478,27 @@
         for copy in edge_copy(0):
             copy.wait_recv()
 
-    def unpack_forcing(s, c):
-        low = pl.ds(pl.multiple_of(s * 8 + 8, 8), 8)
-        high = pl.ds(pl.multiple_of(s * 8 + 8 + R // 2, 8), 8)
-        there = pl.ds(pl.multiple_of(s * 8 + 8 * strip0, 8), 8)
-        halves = []
-        for part in (RSP[s], RSP[s + G // 2]):
-            halves.append(jnp.concatenate([part, roll(part, 64)], axis=0))
+    def unpack_forcing(c, carry):
+        low, high, there = strip_places(c)
+        halves = [[], []]
+        for t in range(SU):
+            for g in range(2):
+                part = RSP[c * SU + t + g * (G // 2)]
+                halves[g] += [part, roll(part, 64)]
+        packed = [jnp.concatenate(parts, axis=0) for parts in halves]
         for f in range(4):
             pieces = []
             for g, rows in ((0, low), (1, high)):
                 at = 48 * g
                 x = F[f, rows, :]
-                pieces.append((halves[g], at - 16 * f, at, at + 8))
+                pieces.append((packed[g], at - 16 * f, at, at + 8))
                 pieces.append((x, at + 8, at + 8, at + 24))
                 pieces.append((x, at + 24 - 112, at + 24, at + 40))
-                pieces.append((halves[g], at + 40 - 16 * f - 8, at + 40, at + 48))
+                pieces.append((packed[g], at + 40 - 16 * f - 8, at + 40, at + 48))
             F[f, there, :] = placed(pieces)
-        return c
-
-    lax.fori_loop(0, S, unpack_forcing, 0)
+        return carry
+
+    lax.fori_loop(0, S // SU, unpack_forcing, 0)
 
     sums = [velocity_sweep(True)]
     stress_sweep()
@@ -489,13 +533,13 @@
         new_u, new_v, total = new_velocity(row, rows_last, False)
         new_u = merged(new_u, U, strip_rows, g)
         new_v = merged(new_v, V, strip_rows, g)
-        VO[0, out, :] = new_u
-        VO[1, out, :] = new_v
+        vel_out[0, out, :] = new_u
+        vel_out[1, out, :] = new_v
         a = merged(X[A, rows, :], A, strip_rows, g)
         b = merged(X[B, rows, :], B, strip_rows, g)
-        SO[0, out, :] = 2.0 * (a + b)
-        SO[1, out, :] = 2.0 * (a - b)
-        SO[2, out, :] = 2.0 * merged(X[C, rows, :], C, strip_rows, g)
+        stress_out[0, out, :] = 2.0 * (a + b)
+        stress_out[1, out, :] = 2.0 * (a - b)
+        stress_out[2, out, :] = 2.0 * merged(X[C, rows, :], C, strip_rows, g)
         ou = F[OU, rows, :]
         ov = F[OV, rows, :]
         drag = drag_of(new_u, new_v, ou, ov) * X[ICE, rows, :]
@@ -522,8 +566,6 @@
         out_copy(k).start()
         return c
 
-    lax.fori_loop(1, G, send_out, 0)
-
     lane = lane_iota(1)
     row = jnp.zeros((1, 128), jnp.float32)
     for k, acc in enumerate(sums):
@@ -548,10 +590,10 @@
 
     lax.fori_loop(1, G, send_x, 0)
 
+    lax.fori_loop(1, G, send_out, 0)
+
     stores = [
-        pltpu.make_async_copy(VO, vel_out, st.at[0]),
-        pltpu.make_async_copy(SO, stress_out, st.at[1]),
-        pltpu.make_async_copy(IST.at[gx], ocean_out.at[:, :, columns(gx)], st.at[2]),
+        pltpu.make_async_copy(IST.at[gx], ocean_out.at[:, :, columns(gx)], st.at[0]),
     ]
     for store in stores:
         store.start()
@@ -583,8 +625,7 @@
 
     lax.fori_loop(1, H, wait_sum_y, 0)
     over_all = jnp.sum(R2R[...], axis=0)
-    for k in range(ITERS):
-        res_out[k] = over_all[0, k]
+    res_out[...] = over_all
 
     def end_forcing(k, c):
         for copy in forcing_copy(k):
@@ -613,6 +654,23 @@
     lax.fori_loop(1, G, end_out, 0)
     for store in stores:
         store.wait()
+
+
+def write_out(
+    vel_ref, stress_ref, res_ref, ocean_ref, vel_out, stress_out, res_out, ocean_out, row, sems
+):
+    copies = [
+        pltpu.make_async_copy(src, dst, sems.at[k])
+        for k, (src, dst) in enumerate(
+            ((res_ref, row), (vel_ref, vel_out), (stress_ref, stress_out), (ocean_ref, ocean_out)))
+    ]
+    for copy in copies:
+        copy.start()
+    copies[0].wait()
+    for k in range(ITERS):
+        res_out[k] = row[0, k]
+    for copy in copies[1:]:
+        copy.wait()
 
 
 def local(G, H, velocity, stress, ice_mass, strength, land_mask, ocean_forcing):
@@ -622,17 +680,15 @@
     rows = 8 * (T + 5 + S)
     f32 = jnp.float32
     anywhere = pl.BlockSpec(memory_space=pl.ANY)
+    in_hbm = pl.BlockSpec(memory_space=pltpu.HBM)
     dma = pltpu.SemaphoreType.DMA
-    return pl.pallas_call(
+    in_vmem = pl.BlockSpec(memory_space=pltpu.VMEM)
+    shapes = ((2, R, 128), (3, R, 128), (1, 128), (2, 8, 128 * G))
+    results = pl.pallas_call(
         functools.partial(kernel, G, H),
-        out_shape=(
-            jax.ShapeDtypeStruct((2, R, 128), f32),
-            jax.ShapeDtypeStruct((3, R, 128), f32),
-            jax.ShapeDtypeStruct((ITERS,), f32),
-            jax.ShapeDtypeStruct((2, 8, 128 * G), f32),
-        ),
-        in_specs=[anywhere] * 6,
-        out_specs=(anywhere, anywhere, pl.BlockSpec(memory_space=pltpu.SMEM), anywhere),
+        out_shape=tuple(pltpu.VMEM(shape, f32) for shape in shapes),
+        in_specs=[in_hbm] * 6,
+        out_specs=(in_vmem,) * 4,
         scratch_shapes=[
             pltpu.VMEM((8, rows, 128), f32),
             pltpu.VMEM((4, rows, 128), f32),
@@ -646,19 +702,29 @@
             pltpu.VMEM((G + 2, 4, 128), f32),
             pltpu.VMEM((2, 8 * S, 128), f32),
             pltpu.VMEM((2, 8 * S, 128), f32),
-            pltpu.VMEM((2, R, 128), f32),
-            pltpu.VMEM((3, R, 128), f32),
+            pltpu.VMEM((4, 8, 128), f32),
+            pltpu.VMEM((4, 8, 128), f32),
             pltpu.VMEM((G, 2, 8, 128), f32),
             pltpu.VMEM((1, 128), f32),
             pltpu.VMEM((G, 1, 128), f32),
             pltpu.VMEM((1, 128), f32),
             pltpu.VMEM((H, 1, 128), f32),
             dma((6,)), dma((G,)), dma((G,)), dma((G,)), dma((G,)),
-            dma((2,)), dma((2,)), dma((2,)), dma((2,)), dma((4,)), dma((4,)),
-            dma((G,)), dma((G,)), dma((G,)), dma((G,)), dma((H,)), dma((H,)), dma((3,)),
+            dma((2,)), dma((2,)), dma((2,)), dma((2,)), dma((4,)), dma((4,)), dma((4,)), dma((4,)),
+            dma((G,)), dma((G,)), dma((G,)), dma((G,)), dma((H,)), dma((H,)), dma((1,)),
         ],
-        compiler_params=pltpu.CompilerParams(collective_id=0, has_side_effects=True),
+        compiler_params=pltpu.CompilerParams(
+            collective_id=0, has_side_effects=True, vmem_limit_bytes=63 * 1024 * 1024),
     )(velocity, stress, ice_mass, strength, land_mask, ocean_forcing)
+    return pl.pallas_call(
+        write_out,
+        out_shape=tuple(
+            jax.ShapeDtypeStruct(shape, f32) for shape in (shapes[0], shapes[1], (ITERS,), shapes[3])),
+        in_specs=[anywhere] * 4,
+        out_specs=(in_hbm, in_hbm, pl.BlockSpec(memory_space=pltpu.SMEM), in_hbm),
+        scratch_shapes=[pltpu.VMEM((1, 128), f32), dma((4,))],
+        compiler_params=pltpu.CompilerParams(vmem_limit_bytes=1024 * 1024),
+    )(*results)
 
 
 def solution(mesh):

time: 66 us -> 51.4 us (0.78)
  Pallas kernels: 61.5 us -> 50.6 us
  local copies, waits for them, and re-layouts: 3.69 us -> 0 us
    pallas_call x1 -> x2, Pallas kernels: 61.5 us -> 50.6 us  [the longest x1 49.1 us: local(): pl.pallas_call(functools.partial(kernel, G, H), out_shape=tuple((pltpu.VM...]
    unnamed x10 -> x0, local copies, waits for them, and re-layouts: 3.69 us -> none
where the time goes in v2:
time: 51.4 us; the launch traced here: 51.2 us
  Pallas kernels  50.6 us (98%)
  between operations  0.64 us (1%)
    pallas_call x1, Pallas kernels, local(): pl.pallas_call(functools.partial(kernel, G, H), out_shape=tuple((pltpu.VM...  49.1 us
    pallas_call x1, Pallas kernels, local(): pl.pallas_call(write_out, out_shape=tuple((jax.ShapeDtypeStruct(shape, f3...  1.47 us

profile of v2, /device:TPU:1, one launch (start us, length us, event | category | flops | bytes accessed | tf_op | source)
XLA Modules:
  0.0 51.2 jit_solution(970003109568923394)
XLA Ops:
  0.6 49.1 %shard_map.93 = (f32[2,256,128]{2,1,0:T(8,128)S(1)}, f32[3,256,128]{2,1,0:T(8,128)S(1)}, f32[1,128]{1,0:T(1,128)S(1)}, f32[2,8,4096]{2,1,0:T(8,128)S(1)}) custom-call(f32[2,256,128]{2,1,0:T(8,128)} %vel_ref.1, f32[3,256,128]{2,1,0:T(8,128)} %stress_ref.1, f32[256,128]{1,0:T(8,128)} %mass_ref.1, f32[256,128]{1,0:T(8,128)} %strength_ref.1, ...), custom_call_target="tpu_custom_call" | custom-call | tf_op jit(solution)/shard_map/pallas_call | solution.py:687
  49.8 1.5 %shard_map.94 = (f32[2,256,128]{2,1,0:T(8,128)}, f32[3,256,128]{2,1,0:T(8,128)}, f32[4]{0:T(128)}, f32[2,8,4096]{2,1,0:T(8,128)}) custom-call(f32[2,256,128]{2,1,0:T(8,128)S(1)} %get-tuple-element.8.vel_ref, f32[3,256,128]{2,1,0:T(8,128)S(1)} %get-tuple-element.9.stress_ref, f32[1,128]{1,0:T(1,128)S(1)} %get-tuple-element.10.res_ref, ...), custom_call_target="tpu_custom_call" | custom-call | tf_op jit(solution)/shard_map/pallas_call | solution.py:719

commit v3 on v2

v3 whole, which is shorter than its diff:
```python
import functools

import jax
import jax.numpy as jnp
from jax import lax
from jax.experimental import pallas as pl
from jax.experimental.pallas import tpu as pltpu
from jax.sharding import PartitionSpec as P

ITERS = 4
MESH = pl.DeviceIdType.MESH

U, V, A, B, C, Q, M, ICE = range(8)
TX, TY, OU, OV = range(4)


def lane_iota(rows=8):
    return lax.broadcasted_iota(jnp.int32, (rows, 128), 1)


def lanes_between(first, last, rows=8):
    lane = lane_iota(rows)
    return (lane >= first) & (lane < last)


def roll(x, shift):
    return pltpu.roll(x, shift % 128, 1) if shift % 128 else x


def placed(pieces):
    total = 0.0
    for x, shift, first, last in pieces:
        total = jnp.where(lanes_between(first, last, x.shape[0]), roll(x, shift), total)
    return total


def kernel(
    G, H,
    vel_ref, stress_ref, mass_ref, strength_ref, mask_ref, forcing_ref,
    vel_out, stress_out, res_out, ocean_out,
    X, F, BUV, MC, FV, RS, RP, RM, FP, FQ, FC, FD, PK, RK, CS, CR, IST, R1S, R1R, R2S, R2R,
    ld, fs, fr, ss, sr, fcs, fcr, las, lar, lon_s, lon_r, cs, cr, fls, flr, os_, or_, rs, rr, st,
):
    T = G
    S = T // 2 + 2
    R = 8 * T
    NY = H * R
    CH = T // 4
    SU = S // 2
    strip0 = T + 6
    NM = (T + 4) // 4
    low_halo, high_halo = 16, 8 * T + 24
    gx = lax.axis_index("gx")
    gy = lax.axis_index("gy")
    east = lax.rem(gx + 1, G)
    west = lax.rem(gx + G - 1, G)
    north = gy + 1
    south = gy - 1
    has_north = gy < H - 1
    has_south = gy > 0

    def peer_x(k):
        p = gx + k
        return jnp.where(p >= G, p - G, p)

    def over_peers(body, start=1, stop=G):
        def step(k, c):
            body(k)
            return c

        lax.fori_loop(start, stop, step, 0)

    half = min(G // 2 + 3, G - 1)
    home = gx // CH

    def peer_y(k):
        p = gy + k
        return jnp.where(p >= H, p - H, p)

    own = pl.ds(24, R)
    loads = [
        pltpu.make_async_copy(forcing_ref, FV, ld.at[0]),
        pltpu.make_async_copy(vel_ref, X.at[pl.ds(0, 2), own, :], ld.at[1]),
        pltpu.make_async_copy(stress_ref, RS, ld.at[2]),
        pltpu.make_async_copy(mass_ref, X.at[M, own, :], ld.at[3]),
        pltpu.make_async_copy(strength_ref, RP, ld.at[4]),
        pltpu.make_async_copy(mask_ref, RM, ld.at[5]),
    ]
    for load in loads:
        load.start()

    bar = pltpu.get_barrier_semaphore()

    def greet_x(k):
        pl.semaphore_signal(bar, inc=1, device_id=(peer_x(k), gy), device_id_type=MESH)

    def greet_y(k, c):
        pl.semaphore_signal(bar, inc=1, device_id=(gx, peer_y(k)), device_id_type=MESH)
        return c

    over_peers(greet_x)
    lax.fori_loop(1, H, greet_y, 0)

    @pl.when(has_south)
    def _():
        for to in (west, east):
            pl.semaphore_signal(bar, inc=1, device_id=(to, south), device_id_type=MESH)

    @pl.when(has_north)
    def _():
        for to in (west, east):
            pl.semaphore_signal(bar, inc=1, device_id=(to, north), device_id_type=MESH)

    for t in (0, 1, T + 4, T + 5, strip0 + S):
        X[:, 8 * t:8 * t + 8, :] = jnp.zeros((8, 8, 128), jnp.float32)
    for t in (1, T + 4):
        F[:, 8 * t:8 * t + 8, :] = jnp.zeros((4, 8, 128), jnp.float32)
        BUV[:, 8 * t:8 * t + 8, :] = jnp.zeros((2, 8, 128), jnp.float32)

    @pl.when(jnp.logical_not(has_south))
    def _():
        X[:, low_halo:low_halo + 8, :] = jnp.zeros((8, 8, 128), jnp.float32)
        F[:, low_halo:low_halo + 8, :] = jnp.zeros((4, 8, 128), jnp.float32)
        CR[0:2] = jnp.zeros((2, 8, 128), jnp.float32)
        FD[0:2] = jnp.zeros((2, 8, 128), jnp.float32)

    @pl.when(jnp.logical_not(has_north))
    def _():
        X[:, high_halo:high_halo + 8, :] = jnp.zeros((8, 8, 128), jnp.float32)
        F[:, high_halo:high_halo + 8, :] = jnp.zeros((4, 8, 128), jnp.float32)
        CR[2:4] = jnp.zeros((2, 8, 128), jnp.float32)
        FD[2:4] = jnp.zeros((2, 8, 128), jnp.float32)

    own_band = pl.ds(pl.multiple_of(gx * 8 + 24, 8), 8)

    def columns(i):
        return pl.ds(pl.multiple_of(i * 128, 128), 128)

    def lat_copy(way):
        if way == 0:
            src, dst, to = 24, high_halo, south
        else:
            src, dst, to = 8 * T + 16, low_halo, north
        return pltpu.make_async_remote_copy(
            src_ref=X.at[:, pl.ds(src, 8), :], dst_ref=X.at[:, pl.ds(dst, 8), :],
            send_sem=las.at[way], recv_sem=lar.at[way], device_id=(gx, to), device_id_type=MESH)

    def corner_copy(n):
        return pltpu.make_async_remote_copy(
            src_ref=CS.at[n], dst_ref=CR.at[n], send_sem=cs.at[n], recv_sem=cr.at[n],
            device_id=(east if n % 2 else west, north if n < 2 else south), device_id_type=MESH)

    def lon_copy(way):
        return pltpu.make_async_remote_copy(
            src_ref=PK.at[way], dst_ref=RK.at[way],
            send_sem=lon_s.at[way], recv_sem=lon_r.at[way],
            device_id=(west if way == 0 else east, gy), device_id_type=MESH)

    arrival = jnp.where(gx == 0, 4, jnp.where(gx == G - 1, 5, home))

    def forcing_copy(k):
        p = peer_x(k)
        return pltpu.make_async_remote_copy(
            src_ref=FV.at[:, :, columns(p)], dst_ref=F.at[:, own_band, :],
            send_sem=fs.at[0], recv_sem=fr.at[arrival], device_id=(p, gy), device_id_type=MESH)

    for load in loads[1:]:
        load.wait()

    def derive(i, c):
        rows = pl.ds(pl.multiple_of(i * 8 * CH, 8), 8 * CH)
        wide = pl.ds(pl.multiple_of(i * 8 * CH + 24, 8), 8 * CH)
        ice = RM[rows, :].astype(jnp.float32)
        quarter = 0.25 * ice
        s0 = RS[0, rows, :]
        s1 = RS[1, rows, :]
        X[A, wide, :] = (s0 + s1) * quarter
        X[B, wide, :] = (s0 - s1) * quarter
        X[C, wide, :] = (RS[2, rows, :] * 0.5) * ice
        X[Q, wide, :] = (RP[rows, :] * 0.0625) * ice
        X[ICE, wide, :] = ice
        return c

    lax.fori_loop(0, T // CH, derive, 0)

    def edge_columns(groups):
        to_west, to_east = [], []
        for g, rows in groups:
            for f in range(8):
                base = 64 * g + 8 * f
                x = X[f, rows, :]
                to_west.append((x, base, base, base + 8))
                to_east.append((x, base + 8, base, base + 8))
        return placed(to_west), placed(to_east)

    def pack_columns(c, carry):
        low = pl.ds(pl.multiple_of(c * 8 * CH + 24, 8), 8 * CH)
        high = pl.ds(pl.multiple_of(c * 8 * CH + 24 + R // 2, 8), 8 * CH)
        here = pl.ds(pl.multiple_of(c * 8 * CH + 8, 8), 8 * CH)
        PK[0, here, :], PK[1, here, :] = edge_columns(((0, low), (1, high)))
        return carry

    lax.fori_loop(0, 2, pack_columns, 0)
    first, last = pl.ds(0, 8), pl.ds(8 * S - 8, 8)
    PK[0, first, :], PK[1, first, :] = edge_columns(((1, pl.ds(16 + R // 2, 8)),))
    PK[0, last, :], PK[1, last, :] = edge_columns(((0, pl.ds(24 + R // 2, 8)),))
    CS[0], CS[1] = edge_columns(((0, pl.ds(8 * T + 16, 8)),))
    CS[2], CS[3] = edge_columns(((1, pl.ds(24, 8)),))

    loads[0].wait()
    for f in range(4):
        F[f, own_band, :] = FV[f, :, columns(gx)]

    diagonal = 2 * has_south.astype(jnp.int32) + 2 * has_north.astype(jnp.int32)
    pl.semaphore_wait(bar, G - 1 + H - 1 + diagonal)

    lon_copy(0).start()
    lon_copy(1).start()

    @pl.when(has_south)
    def _():
        lat_copy(0).start()
        corner_copy(2).start()
        corner_copy(3).start()

    @pl.when(has_north)
    def _():
        lat_copy(1).start()
        corner_copy(0).start()
        corner_copy(1).start()

    over_peers(lambda k: forcing_copy(k).start())

    @pl.when(has_south)
    def _():
        lat_copy(1).wait_recv()
        corner_copy(0).wait_recv()
        corner_copy(1).wait_recv()

    @pl.when(has_north)
    def _():
        lat_copy(0).wait_recv()
        corner_copy(2).wait_recv()
        corner_copy(3).wait_recv()

    band0 = gy * R

    def coriolis(first_row, half, count):
        row = first_row + lax.broadcasted_iota(jnp.int32, (count, 128), 0)
        if half:
            row = row + jnp.where(lane_iota(count) >= 48, half, 0)
        return 0.3 + 1.2 * (row.astype(jnp.float32) + 0.5) / NY

    def main_coriolis(t, c):
        rows = pl.ds(pl.multiple_of(t * 8 * NM + 8, 8), 8 * NM)
        MC[rows, :] = X[M, rows, :] * coriolis(band0 + t * 8 * NM - 16, 0, 8 * NM)
        return c

    lax.fori_loop(0, 4, main_coriolis, 0)
    for way in range(2):
        lon_copy(way).wait()
        RK[way, 0:8, :] = jnp.where(lanes_between(0, 64), CR[way], RK[way, 0:8, :])
        RK[way, 8 * S - 8:8 * S, :] = jnp.where(
            lanes_between(64, 128), CR[way + 2], RK[way, 8 * S - 8:8 * S, :])

    def strip_tile(own_low, own_high, from_west, west_shifts, from_east, east_shifts):
        pieces = []
        for g, x in ((0, own_low), (1, own_high)):
            at = 48 * g
            pieces.append((from_west, at - west_shifts[g], at, at + 8))
            pieces.append((x, at + 8, at + 8, at + 24))
            pieces.append((x, at + 24 - 112, at + 24, at + 40))
            pieces.append((from_east, at + 40 - east_shifts[g], at + 40, at + 48))
        return placed(pieces)

    def strip_places(c):
        low = pl.ds(pl.multiple_of(c * 8 * SU + 16, 8), 8 * SU)
        high = pl.ds(pl.multiple_of(c * 8 * SU + 16 + R // 2, 8), 8 * SU)
        there = pl.ds(pl.multiple_of(c * 8 * SU + 8 * strip0, 8), 8 * SU)
        return low, high, there

    def unpack_columns(c, carry):
        low, high, there = strip_places(c)
        here = pl.ds(pl.multiple_of(c * 8 * SU, 8), 8 * SU)
        from_east = RK[0, here, :]
        from_west = RK[1, here, :]
        for f in range(8):
            shifts = (8 * f, 64 + 8 * f)
            x = strip_tile(X[f, low, :], X[f, high, :], from_west, shifts, from_east, shifts)
            X[f, there, :] = x
            if f == M:
                MC[there, :] = x * coriolis(band0 + c * 8 * SU - 8, R // 2, 8 * SU)
        return carry

    lax.fori_loop(0, 2, unpack_columns, 0)

    @pl.when(has_south)
    def _():
        lat_copy(0).wait_send()
        corner_copy(2).wait_send()
        corner_copy(3).wait_send()

    @pl.when(has_north)
    def _():
        lat_copy(1).wait_send()
        corner_copy(0).wait_send()
        corner_copy(1).wait_send()

    def relax_stress(row, count):
        rows = pl.ds(row, count)
        up = pl.ds(row + 1, count)
        down = pl.ds(row - 1, count)
        u = X[U, rows, :]
        v = X[V, rows, :]
        east_dx = roll(u, -1) - roll(u, 1)
        north_dx = roll(v, -1) - roll(v, 1)
        east_dy = X[U, up, :] - X[U, down, :]
        north_dy = X[V, up, :] - X[V, down, :]
        tension = east_dx - north_dy
        shear = east_dy + north_dx
        g = 2.0 * (east_dx + north_dy)
        h = 0.5 * tension
        inverse = lax.rsqrt(g * g + (tension * tension + shear * shear) + 0.04)
        q = X[Q, rows, :]
        qr = q * inverse
        X[A, rows, :] = 0.75 * X[A, rows, :] + ((g + h) * qr - q)
        X[B, rows, :] = 0.75 * X[B, rows, :] + ((g - h) * qr - q)
        X[C, rows, :] = 0.75 * X[C, rows, :] + (0.5 * shear) * qr

    def drag_of(u, v, ou, ov):
        du = ou - u
        dv = ov - v
        square = du * du + dv * dv + 0.01
        return square * lax.rsqrt(square)

    def new_velocity(row, count, first):
        rows = pl.ds(row, count)
        up = pl.ds(row + 1, count)
        down = pl.ds(row - 1, count)
        a = X[A, rows, :]
        c = X[C, rows, :]
        force_east = (roll(a, -1) - roll(a, 1)) + (X[C, up, :] - X[C, down, :])
        force_north = (roll(c, -1) - roll(c, 1)) + (X[B, up, :] - X[B, down, :])
        u = X[U, rows, :]
        v = X[V, rows, :]
        ou = F[OU, rows, :]
        ov = F[OV, rows, :]
        m = X[M, rows, :]
        mc = MC[rows, :]
        if first:
            bu = m * u + F[TX, rows, :]
            bv = m * v + F[TY, rows, :]
            BUV[0, rows, :] = bu
            BUV[1, rows, :] = bv
        else:
            bu = BUV[0, rows, :]
            bv = BUV[1, rows, :]
        drag = drag_of(u, v, ou, ov)
        m4 = 4.0 * m
        w = X[ICE, rows, :] / (m4 + m + drag)
        new_u = (m4 * u + mc * v + (bu + force_east + drag * ou)) * w
        new_v = (m4 * v - mc * u + (bv + force_north + drag * ov)) * w
        du = new_u - u
        dv = new_v - v
        return new_u, new_v, du * du + dv * dv

    def tile_sum(change, weight=lambda t: None):
        total = None
        for t in range(change.shape[0] // 8):
            tile = change[8 * t:8 * t + 8]
            scale = weight(t)
            if scale is not None:
                tile = tile * scale
            total = tile if total is None else total + tile
        return total

    main_lanes = lanes_between(8, 120)
    strip_lanes = (
        lanes_between(8, 16) | lanes_between(32, 40) | lanes_between(56, 64) | lanes_between(80, 88))
    zero = jnp.zeros((8, 128), jnp.float32)

    def both_sums(main, strip):
        return jnp.where(main_lanes, main, 0.0) + jnp.where(strip_lanes, strip, 0.0)

    main_region = (1, T + 4, 4)
    strip_region = (strip0, S, 2)

    def part_row(region, c):
        first, tiles, parts = region
        return pl.multiple_of(8 * first + c * (8 * tiles // parts), 8), tiles // parts

    def stress_sweep(region):
        def body(c, carry):
            row, tiles = part_row(region, c)
            relax_stress(row, 8 * tiles)
            return carry

        lax.fori_loop(0, region[2], body, 0)

    def velocity_sweep(region, first):
        _, all_tiles, parts = region
        edge = (all_tiles - (T if region is main_region else T // 2)) // 2

        def body(c, acc):
            row, tiles = part_row(region, c)
            rows = pl.ds(row, 8 * tiles)
            new_u, new_v, change = new_velocity(row, 8 * tiles, first)
            X[U, rows, :] = new_u
            X[V, rows, :] = new_v

            def weight(t):
                if edge <= t < tiles - edge:
                    return None
                inside = jnp.bool_(True)
                if t < edge:
                    inside = c > 0
                if t >= tiles - edge:
                    inside = inside & (c < parts - 1)
                return jnp.where(inside, 1.0, 0.0)

            return acc + tile_sum(change, weight)

        return lax.fori_loop(0, parts, body, zero)

    stress_sweep(main_region)
    stress_sweep(strip_region)

    def wait_bands(sem, row, count):
        where = F.at[:, pl.ds(row, 8 * count), :]
        pltpu.make_async_copy(where, where, fr.at[sem]).wait()

    def edge_copy(way):
        if way == 0:
            src, dst, to = 24, high_halo, south
        else:
            src, dst, to = 8 * T + 16, low_halo, north
        return pltpu.make_async_remote_copy(
            src_ref=F.at[:, pl.ds(src, 8), :], dst_ref=F.at[:, pl.ds(dst, 8), :],
            send_sem=fls.at[way], recv_sem=flr.at[way], device_id=(gx, to), device_id_type=MESH)

    def edge_corner_copy(n):
        return pltpu.make_async_remote_copy(
            src_ref=FC.at[n], dst_ref=FD.at[n], send_sem=fcs.at[n], recv_sem=fcr.at[n],
            device_id=(east if n % 2 else west, north if n < 2 else south), device_id_type=MESH)

    def side_copy(way):
        return pltpu.make_async_remote_copy(
            src_ref=FP.at[way], dst_ref=FQ.at[way], send_sem=ss.at[way], recv_sem=sr.at[way],
            device_id=(west if way == 0 else east, gy), device_id_type=MESH)

    def forcing_columns(rows):
        to_west, to_east = [], []
        for f in range(4):
            x = F[f, rows, :]
            to_west.append((x, 8 * f, 8 * f, 8 * f + 8))
            to_east.append((x, 8 * f + 8, 8 * f, 8 * f + 8))
        return placed(to_west), placed(to_east)

    def pass_on(first):
        sem, edge, here, way = (4, 0, has_south, 0) if first else (5, G - 1, has_north, 1)
        row = 8 * edge + 24
        corners = (2, 3) if first else (0, 1)

        @pl.when(gx != edge)
        def _():
            wait_bands(sem, row, 1)

        @pl.when(here)
        def _():
            edge_copy(way).start()
            FC[corners[0]], FC[corners[1]] = forcing_columns(pl.ds(row, 8))
            edge_corner_copy(corners[0]).start()
            edge_corner_copy(corners[1]).start()

    def first_velocity(row, count):
        new_u, new_v, change = new_velocity(row, count, True)
        X[U, pl.ds(row, count), :] = new_u
        X[V, pl.ds(row, count), :] = new_v
        return tile_sum(change)

    FP[...] = jnp.zeros((2, 8 * CH, 128), jnp.float32)
    at_home = jnp.where((gx == 0) | (gx == G - 1), 0, 1)

    def receive(step, acc):
        @pl.when(step == jnp.maximum(home - 1, 0))
        def _():
            pass_on(True)

        @pl.when(step == home)
        def _():
            pass_on(False)

        chunk = home + 3 - step
        chunk = jnp.where(chunk >= 4, chunk - 4, chunk)
        row = pl.multiple_of(chunk * 8 * CH + 24, 8)
        missing = (
            jnp.where(chunk == 0, 1, 0) + jnp.where(chunk == 3, 1, 0)
            + jnp.where(chunk == home, at_home, 0))
        for count in range(max(CH - 2, 1), CH + 1):
            @pl.when(missing == CH - count)
            def _():
                wait_bands(chunk, row, count)

        in_chunk = lane_iota(8 * CH) // 32 == chunk
        for way, x in enumerate(forcing_columns(pl.ds(row, 8 * CH))):
            FP[way] = jnp.where(in_chunk, pltpu.roll(x, chunk * 32, 1), FP[way])

        @pl.when(step == 3)
        def _():
            side_copy(0).start()
            side_copy(1).start()

        return acc + first_velocity(row, 8 * CH)

    main_sum = lax.fori_loop(0, 4, receive, zero)

    @pl.when(has_south)
    def _():
        edge_copy(1).wait_recv()

    @pl.when(has_north)
    def _():
        edge_copy(0).wait_recv()

    first_velocity(low_halo, 8)
    first_velocity(high_halo, 8)

    main_sums = [main_sum]
    stress_sweep(main_region)
    main_sums.append(velocity_sweep(main_region, False))
    stress_sweep(main_region)
    main_sums.append(velocity_sweep(main_region, False))
    stress_sweep(main_region)
    main_sums.append(velocity_sweep(main_region, False))

    def unpack_own(c, carry):
        low, high, there = strip_places(c)
        for f in range(4):
            pieces = []
            for g, rows in ((0, low), (1, high)):
                at = 48 * g
                x = F[f, rows, :]
                pieces.append((x, at + 8, at + 8, at + 24))
                pieces.append((x, at + 24 - 112, at + 24, at + 40))
            F[f, there, :] = placed(pieces)
        return carry

    lax.fori_loop(0, 2, unpack_own, 0)

    def unpack_sides(row, count, left, right, shifts):
        for f in range(4):
            x = F[f, pl.ds(row, count), :]
            for g in range(2):
                at = 48 * g
                lanes = shifts[g] + 8 * f
                x = jnp.where(lanes_between(at, at + 8, count), roll(left[g], at - lanes), x)
                x = jnp.where(
                    lanes_between(at + 40, at + 48, count), roll(right[g], at + 40 - lanes), x)
            F[f, pl.ds(row, count), :] = x

    side_copy(0).wait()
    side_copy(1).wait()

    @pl.when(has_south)
    def _():
        edge_corner_copy(0).wait_recv()
        edge_corner_copy(1).wait_recv()

    @pl.when(has_north)
    def _():
        edge_corner_copy(2).wait_recv()
        edge_corner_copy(3).wait_recv()

    for half_rows in range(2):
        unpack_sides(
            8 * strip0 + 8 + half_rows * 8 * CH, 8 * CH,
            (FQ[1], FQ[1]), (FQ[0], FQ[0]), (32 * half_rows, 32 * half_rows + 64))
    unpack_sides(
        8 * strip0, 8,
        (FD[1], FQ[1, 8 * CH - 8:8 * CH]), (FD[0], FQ[0, 8 * CH - 8:8 * CH]), (0, 32))
    unpack_sides(
        8 * (strip0 + S - 1), 8, (FQ[1, 0:8], FD[3]), (FQ[0, 0:8], FD[2]), (64, 0))

    strip_sums = [velocity_sweep(strip_region, True)]
    stress_sweep(strip_region)
    strip_sums.append(velocity_sweep(strip_region, False))
    stress_sweep(strip_region)
    strip_sums.append(velocity_sweep(strip_region, False))
    stress_sweep(strip_region)
    strip_sums.append(velocity_sweep(strip_region, False))
    sums = [both_sums(main, strip) for main, strip in zip(main_sums, strip_sums)]

    lane = lane_iota(1)
    row = jnp.zeros((1, 128), jnp.float32)
    for k, acc in enumerate(sums):
        total = jnp.sum(jnp.sum(acc, axis=0, keepdims=True), axis=1, keepdims=True)
        row = jnp.where(lane == k, total, row)
    R2S[...] = row
    R2R[gy] = row

    def sum_copy_y(k):
        return pltpu.make_async_remote_copy(
            src_ref=R2S, dst_ref=R2R.at[gy],
            send_sem=rs.at[0], recv_sem=rr.at[0], device_id=(gx, peer_y(k)), device_id_type=MESH)

    def sum_copy_x(k):
        return pltpu.make_async_remote_copy(
            src_ref=R1S, dst_ref=R1R.at[gx],
            send_sem=rs.at[1], recv_sem=rr.at[1], device_id=(peer_x(k), gy), device_id_type=MESH)

    def wait_all(ref, count, sems):
        for sem in sems:
            pltpu.make_async_copy(ref.at[pl.ds(0, count)], ref.at[pl.ds(0, count)], sem).wait()

    def send_y(k, c):
        sum_copy_y(k).start()
        return c

    lax.fori_loop(1, H, send_y, 0)

    rows_last = 8 * CH
    left = lanes_between(0, 8, rows_last)
    right = lanes_between(120, 128, rows_last)

    def merged(x, f, strip_rows, g):
        strip = X[f, strip_rows, :]
        x = jnp.where(left, roll(strip, -(48 * g + 8)), x)
        return jnp.where(right, roll(strip, 88 - 48 * g), x)

    def last_main(g, c, carry):
        first = pl.multiple_of(c * 8 * CH + g * R // 2, 8)
        row = pl.multiple_of(first + 24, 8)
        rows = pl.ds(row, rows_last)
        out = pl.ds(first, rows_last)
        strip_rows = pl.ds(pl.multiple_of((strip0 + 1) * 8 + c * 8 * CH, 8), rows_last)
        new_u = merged(X[U, rows, :], U, strip_rows, g)
        new_v = merged(X[V, rows, :], V, strip_rows, g)
        vel_out[0, out, :] = new_u
        vel_out[1, out, :] = new_v
        ou = F[OU, rows, :]
        ov = F[OV, rows, :]
        drag = drag_of(new_u, new_v, ou, ov) * X[ICE, rows, :]
        east_stress = drag * (new_u - ou)
        north_stress = drag * (new_v - ov)
        for t in range(CH):
            band = c * CH + g * (T // 2) + t
            IST[band, 0] = east_stress[8 * t:8 * t + 8]
            IST[band, 1] = north_stress[8 * t:8 * t + 8]
        return carry

    def last_stress(g, c, carry):
        first = pl.multiple_of(c * 8 * CH + g * R // 2, 8)
        rows = pl.ds(pl.multiple_of(first + 24, 8), rows_last)
        out = pl.ds(first, rows_last)
        strip_rows = pl.ds(pl.multiple_of((strip0 + 1) * 8 + c * 8 * CH, 8), rows_last)
        a = merged(X[A, rows, :], A, strip_rows, g)
        b = merged(X[B, rows, :], B, strip_rows, g)
        stress_out[0, out, :] = 2.0 * (a + b)
        stress_out[1, out, :] = 2.0 * (a - b)
        stress_out[2, out, :] = 2.0 * merged(X[C, rows, :], C, strip_rows, g)
        return carry

    for g in range(2):
        lax.fori_loop(0, 2, functools.partial(last_main, g), 0)

    def out_copy(k):
        p = peer_x(k)
        return pltpu.make_async_remote_copy(
            src_ref=IST.at[p], dst_ref=ocean_out.at[:, :, columns(gx)],
            send_sem=os_.at[0], recv_sem=or_.at[0], device_id=(p, gy), device_id_type=MESH)

    over_peers(lambda k: out_copy(k).start(), 1, half)
    stores = [
        pltpu.make_async_copy(IST.at[gx], ocean_out.at[:, :, columns(gx)], st.at[0]),
    ]
    for store in stores:
        store.start()

    for g in range(2):
        lax.fori_loop(0, 2, functools.partial(last_stress, g), 0)

    wait_all(R2R, H - 1, (rs.at[0], rr.at[0]))
    over_y = jnp.sum(R2R[...], axis=0)
    R1S[...] = over_y
    R1R[gx] = over_y

    over_peers(lambda k: sum_copy_x(k).start())
    over_peers(lambda k: out_copy(k).start(), half, G)

    wait_all(R1R, G - 1, (rs.at[1], rr.at[1]))
    res_out[...] = jnp.sum(R1R[...], axis=0)

    sent = F.at[:, pl.ds(24, R - 8), :]
    pltpu.make_async_copy(sent, sent, fs.at[0]).wait()

    @pl.when(has_south)
    def _():
        edge_copy(0).wait_send()
        edge_corner_copy(2).wait_send()
        edge_corner_copy(3).wait_send()

    @pl.when(has_north)
    def _():
        edge_copy(1).wait_send()
        edge_corner_copy(0).wait_send()
        edge_corner_copy(1).wait_send()

    wait_all(IST, G - 1, (os_.at[0], or_.at[0]))
    for store in stores:
        store.wait()


def write_out(
    vel_ref, stress_ref, res_ref, ocean_ref, vel_out, stress_out, res_out, ocean_out, row, sems
):
    copies = [
        pltpu.make_async_copy(src, dst, sems.at[k])
        for k, (src, dst) in enumerate(
            ((res_ref, row), (vel_ref, vel_out), (stress_ref, stress_out), (ocean_ref, ocean_out)))
    ]
    for copy in copies:
        copy.start()
    copies[0].wait()
    for k in range(ITERS):
        res_out[k] = row[0, k]
    for copy in copies[1:]:
        copy.wait()


def local(G, H, velocity, stress, ice_mass, strength, land_mask, ocean_forcing):
    T = G
    S = T // 2 + 2
    R = 8 * T
    rows = 8 * (T + 7 + S)
    f32 = jnp.float32
    anywhere = pl.BlockSpec(memory_space=pl.ANY)
    in_hbm = pl.BlockSpec(memory_space=pltpu.HBM)
    dma = pltpu.SemaphoreType.DMA
    in_vmem = pl.BlockSpec(memory_space=pltpu.VMEM)
    shapes = ((2, R, 128), (3, R, 128), (1, 128), (2, 8, 128 * G))
    results = pl.pallas_call(
        functools.partial(kernel, G, H),
        out_shape=tuple(pltpu.VMEM(shape, f32) for shape in shapes),
        in_specs=[in_hbm] * 6,
        out_specs=(in_vmem,) * 4,
        scratch_shapes=[
            pltpu.VMEM((8, rows, 128), f32),
            pltpu.VMEM((4, rows, 128), f32),
            pltpu.VMEM((2, rows, 128), f32),
            pltpu.VMEM((rows, 128), f32),
            pltpu.VMEM((4, 8, 128 * G), f32),
            pltpu.VMEM((3, R, 128), f32),
            pltpu.VMEM((R, 128), f32),
            pltpu.VMEM((R, 128), jnp.int32),
            pltpu.VMEM((2, 2 * T, 128), f32),
            pltpu.VMEM((2, 2 * T, 128), f32),
            pltpu.VMEM((4, 8, 128), f32),
            pltpu.VMEM((4, 8, 128), f32),
            pltpu.VMEM((2, 8 * S, 128), f32),
            pltpu.VMEM((2, 8 * S, 128), f32),
            pltpu.VMEM((4, 8, 128), f32),
            pltpu.VMEM((4, 8, 128), f32),
            pltpu.VMEM((G, 2, 8, 128), f32),
            pltpu.VMEM((1, 128), f32),
            pltpu.VMEM((G, 1, 128), f32),
            pltpu.VMEM((1, 128), f32),
            pltpu.VMEM((H, 1, 128), f32),
            dma((6,)), dma((1,)), dma((6,)), dma((2,)), dma((2,)), dma((4,)), dma((4,)),
            dma((2,)), dma((2,)), dma((2,)), dma((2,)), dma((4,)), dma((4,)), dma((2,)), dma((2,)),
            dma((1,)), dma((1,)), dma((2,)), dma((2,)), dma((1,)),
        ],
        compiler_params=pltpu.CompilerParams(
            collective_id=0, has_side_effects=True, vmem_limit_bytes=63 * 1024 * 1024),
    )(velocity, stress, ice_mass, strength, land_mask, ocean_forcing)
    return pl.pallas_call(
        write_out,
        out_shape=tuple(
            jax.ShapeDtypeStruct(shape, f32) for shape in (shapes[0], shapes[1], (ITERS,), shapes[3])),
        in_specs=[anywhere] * 4,
        out_specs=(in_hbm, in_hbm, pl.BlockSpec(memory_space=pltpu.SMEM), in_hbm),
        scratch_shapes=[pltpu.VMEM((1, 128), f32), dma((4,))],
        compiler_params=pltpu.CompilerParams(vmem_limit_bytes=1024 * 1024),
    )(*results)


def solution(mesh):
    block = P(None, "gy", "gx")
    plane = P("gy", "gx")
    bands = P(None, ("gy", "gx"), None)
    return jax.shard_map(
        functools.partial(local, mesh.shape["gx"], mesh.shape["gy"]),
        mesh=mesh,
        in_specs=(block, block, plane, plane, plane, bands),
        out_specs=(block, block, P(), bands),
        check_vma=False,
    )
```

time: 51.4 us -> 48 us (0.934)
  Pallas kernels: 50.6 us -> 47.3 us
    pallas_call x1, Pallas kernels: 49.1 us -> 45.8 us  [local(): pl.pallas_call(functools.partial(kernel, G, H), out_shape=tuple((pltpu.VM...]
where the time goes in v3:
time: 48 us; the launch traced here: 47.9 us
  Pallas kernels  47.3 us (99%)
  between operations  0.64 us (1%)
    pallas_call x1, Pallas kernels, local(): pl.pallas_call(functools.partial(kernel, G, H), out_shape=tuple((pltpu.VM...  45.8 us
    pallas_call x1, Pallas kernels, local(): pl.pallas_call(write_out, out_shape=tuple((jax.ShapeDtypeStruct(shape, f3...  1.47 us

profile of v3, /device:TPU:1, one launch (start us, length us, event | category | flops | bytes accessed | tf_op | source)
XLA Modules:
  0.0 47.9 jit_solution(553461739577069715)
XLA Ops:
  0.6 45.8 %shard_map.93 = (f32[2,256,128]{2,1,0:T(8,128)S(1)}, f32[3,256,128]{2,1,0:T(8,128)S(1)}, f32[1,128]{1,0:T(1,128)S(1)}, f32[2,8,4096]{2,1,0:T(8,128)S(1)}) custom-call(f32[2,256,128]{2,1,0:T(8,128)} %vel_ref.1, f32[3,256,128]{2,1,0:T(8,128)} %stress_ref.1, f32[256,128]{1,0:T(8,128)} %mass_ref.1, f32[256,128]{1,0:T(8,128)} %strength_ref.1, ...), custom_call_target="tpu_custom_call" | custom-call | tf_op jit(solution)/shard_map/pallas_call | solution.py:741
  46.4 1.5 %shard_map.94 = (f32[2,256,128]{2,1,0:T(8,128)}, f32[3,256,128]{2,1,0:T(8,128)}, f32[4]{0:T(128)}, f32[2,8,4096]{2,1,0:T(8,128)}) custom-call(f32[2,256,128]{2,1,0:T(8,128)S(1)} %get-tuple-element.8.vel_ref, f32[3,256,128]{2,1,0:T(8,128)S(1)} %get-tuple-element.9.stress_ref, f32[1,128]{1,0:T(1,128)S(1)} %get-tuple-element.10.res_ref, ...), custom_call_target="tpu_custom_call" | custom-call | tf_op jit(solution)/shard_map/pallas_call | solution.py:775

commit v4 on v3

--- a/solution.py
+++ b/solution.py
@@ -70,7 +70,18 @@
 
         lax.fori_loop(start, stop, step, 0)
 
-    half = min(G // 2 + 3, G - 1)
+    half = G // 2
+
+    def over_all_x(body, start=0, stop=G):
+        def step(p, c):
+            @pl.when(p != gx)
+            def _():
+                body(p)
+
+            return c
+
+        lax.fori_loop(start, stop, step, 0)
+
     home = gx // CH
 
     def peer_y(k):
@@ -188,9 +199,9 @@
         for g, rows in groups:
             for f in range(8):
                 base = 64 * g + 8 * f
-                x = X[f, rows, :]
-                to_west.append((x, base, base, base + 8))
-                to_east.append((x, base + 8, base, base + 8))
+                x = roll(X[f, rows, :], base + 8)
+                to_west.append((x, 0, (base + 8) % 128, (base + 8) % 128 + 8))
+                to_east.append((x, 0, base, base + 8))
         return placed(to_west), placed(to_east)
 
     def pack_columns(c, carry):
@@ -229,7 +240,14 @@
         corner_copy(0).start()
         corner_copy(1).start()
 
-    over_peers(lambda k: forcing_copy(k).start())
+    forcing_copy(G // 2).start()
+
+    def send_pair(m, c):
+        forcing_copy(G // 2 - m).start()
+        forcing_copy(G // 2 + m).start()
+        return c
+
+    lax.fori_loop(1, G // 2, send_pair, 0)
 
     @pl.when(has_south)
     def _():
@@ -259,9 +277,9 @@
     lax.fori_loop(0, 4, main_coriolis, 0)
     for way in range(2):
         lon_copy(way).wait()
-        RK[way, 0:8, :] = jnp.where(lanes_between(0, 64), CR[way], RK[way, 0:8, :])
-        RK[way, 8 * S - 8:8 * S, :] = jnp.where(
-            lanes_between(64, 128), CR[way + 2], RK[way, 8 * S - 8:8 * S, :])
+        lower = lanes_between(8, 72) if way == 0 else lanes_between(0, 64)
+        RK[way, 0:8, :] = jnp.where(lower, CR[way], RK[way, 0:8, :])
+        RK[way, 8 * S - 8:8 * S, :] = jnp.where(lower, RK[way, 8 * S - 8:8 * S, :], CR[way + 2])
 
     def strip_tile(own_low, own_high, from_west, west_shifts, from_east, east_shifts):
         pieces = []
@@ -286,7 +304,8 @@
         from_west = RK[1, here, :]
         for f in range(8):
             shifts = (8 * f, 64 + 8 * f)
-            x = strip_tile(X[f, low, :], X[f, high, :], from_west, shifts, from_east, shifts)
+            rotated = (8 * f + 8, 64 + 8 * f + 8)
+            x = strip_tile(X[f, low, :], X[f, high, :], from_west, shifts, from_east, rotated)
             X[f, there, :] = x
             if f == M:
                 MC[there, :] = x * coriolis(band0 + c * 8 * SU - 8, R // 2, 8 * SU)
@@ -387,12 +406,16 @@
 
     def part_row(region, c):
         first, tiles, parts = region
-        return pl.multiple_of(8 * first + c * (8 * tiles // parts), 8), tiles // parts
+        row = 8 * first + c * (8 * tiles // parts)
+        return row if isinstance(c, int) else pl.multiple_of(row, 8), tiles // parts
+
+    def relax_part(region, c):
+        row, tiles = part_row(region, c)
+        relax_stress(row, 8 * tiles)
 
     def stress_sweep(region):
         def body(c, carry):
-            row, tiles = part_row(region, c)
-            relax_stress(row, 8 * tiles)
+            relax_part(region, c)
             return carry
 
         lax.fori_loop(0, region[2], body, 0)
@@ -451,9 +474,9 @@
     def forcing_columns(rows):
         to_west, to_east = [], []
         for f in range(4):
-            x = F[f, rows, :]
-            to_west.append((x, 8 * f, 8 * f, 8 * f + 8))
-            to_east.append((x, 8 * f + 8, 8 * f, 8 * f + 8))
+            x = roll(F[f, rows, :], 8 * f + 8)
+            to_west.append((x, 0, 8 * f + 8, 8 * f + 16))
+            to_east.append((x, 0, 8 * f, 8 * f + 8))
         return placed(to_west), placed(to_east)
 
     def pass_on(first):
@@ -501,8 +524,10 @@
             def _():
                 wait_bands(chunk, row, count)
 
-        in_chunk = lane_iota(8 * CH) // 32 == chunk
+        lane = lane_iota(8 * CH)
         for way, x in enumerate(forcing_columns(pl.ds(row, 8 * CH))):
+            at = chunk * 32 + (8 if way == 0 else 0)
+            in_chunk = ((lane >= at) & (lane < at + 32)) | (lane < at - 96)
             FP[way] = jnp.where(in_chunk, pltpu.roll(x, chunk * 32, 1), FP[way])
 
         @pl.when(step == 3)
@@ -513,6 +538,24 @@
         return acc + first_velocity(row, 8 * CH)
 
     main_sum = lax.fori_loop(0, 4, receive, zero)
+    def unpack_own(row, count, low, high):
+        for f in range(4):
+            pieces = []
+            for g, rows in ((0, low), (1, high)):
+                at = 48 * g
+                x = F[f, pl.ds(rows, count), :]
+                pieces.append((x, at + 8, at + 8, at + 24))
+                pieces.append((x, at + 24 - 112, at + 24, at + 40))
+            F[f, pl.ds(row, count), :] = placed(pieces)
+
+    for part in range(2):
+        own_row = 24 + part * 8 * CH
+        unpack_own(8 * strip0 + 8 + part * 8 * CH, 8 * CH, own_row, own_row + R // 2)
+
+    inner = (1, 2) if NM > 2 else ()
+    for part in inner:
+        relax_part(main_region, part)
+
 
     @pl.when(has_south)
     def _():
@@ -524,28 +567,18 @@
 
     first_velocity(low_halo, 8)
     first_velocity(high_halo, 8)
+    unpack_own(8 * strip0, 8, low_halo, 16 + R // 2)
+    unpack_own(8 * (strip0 + S - 1), 8, 24 + R // 2, high_halo)
 
     main_sums = [main_sum]
-    stress_sweep(main_region)
+    for part in range(4):
+        if part not in inner:
+            relax_part(main_region, part)
     main_sums.append(velocity_sweep(main_region, False))
     stress_sweep(main_region)
     main_sums.append(velocity_sweep(main_region, False))
     stress_sweep(main_region)
     main_sums.append(velocity_sweep(main_region, False))
-
-    def unpack_own(c, carry):
-        low, high, there = strip_places(c)
-        for f in range(4):
-            pieces = []
-            for g, rows in ((0, low), (1, high)):
-                at = 48 * g
-                x = F[f, rows, :]
-                pieces.append((x, at + 8, at + 8, at + 24))
-                pieces.append((x, at + 24 - 112, at + 24, at + 40))
-            F[f, there, :] = placed(pieces)
-        return carry
-
-    lax.fori_loop(0, 2, unpack_own, 0)
 
     def unpack_sides(row, count, left, right, shifts):
         for f in range(4):
@@ -555,7 +588,7 @@
                 lanes = shifts[g] + 8 * f
                 x = jnp.where(lanes_between(at, at + 8, count), roll(left[g], at - lanes), x)
                 x = jnp.where(
-                    lanes_between(at + 40, at + 48, count), roll(right[g], at + 40 - lanes), x)
+                    lanes_between(at + 40, at + 48, count), roll(right[g], at + 32 - lanes), x)
             F[f, pl.ds(row, count), :] = x
 
     side_copy(0).wait()
@@ -595,28 +628,24 @@
     for k, acc in enumerate(sums):
         total = jnp.sum(jnp.sum(acc, axis=0, keepdims=True), axis=1, keepdims=True)
         row = jnp.where(lane == k, total, row)
-    R2S[...] = row
-    R2R[gy] = row
+    R1S[...] = row
+    R1R[gx] = row
 
     def sum_copy_y(k):
         return pltpu.make_async_remote_copy(
             src_ref=R2S, dst_ref=R2R.at[gy],
             send_sem=rs.at[0], recv_sem=rr.at[0], device_id=(gx, peer_y(k)), device_id_type=MESH)
 
-    def sum_copy_x(k):
+    def sum_copy_x(p):
         return pltpu.make_async_remote_copy(
             src_ref=R1S, dst_ref=R1R.at[gx],
-            send_sem=rs.at[1], recv_sem=rr.at[1], device_id=(peer_x(k), gy), device_id_type=MESH)
+            send_sem=rs.at[1], recv_sem=rr.at[1], device_id=(p, gy), device_id_type=MESH)
 
     def wait_all(ref, count, sems):
         for sem in sems:
             pltpu.make_async_copy(ref.at[pl.ds(0, count)], ref.at[pl.ds(0, count)], sem).wait()
 
-    def send_y(k, c):
-        sum_copy_y(k).start()
-        return c
-
-    lax.fori_loop(1, H, send_y, 0)
+    over_all_x(lambda p: sum_copy_x(p).start())
 
     rows_last = 8 * CH
     left = lanes_between(0, 8, rows_last)
@@ -663,13 +692,12 @@
     for g in range(2):
         lax.fori_loop(0, 2, functools.partial(last_main, g), 0)
 
-    def out_copy(k):
-        p = peer_x(k)
+    def out_copy(p):
         return pltpu.make_async_remote_copy(
             src_ref=IST.at[p], dst_ref=ocean_out.at[:, :, columns(gx)],
             send_sem=os_.at[0], recv_sem=or_.at[0], device_id=(p, gy), device_id_type=MESH)
 
-    over_peers(lambda k: out_copy(k).start(), 1, half)
+    over_all_x(lambda p: out_copy(p).start())
     stores = [
         pltpu.make_async_copy(IST.at[gx], ocean_out.at[:, :, columns(gx)], st.at[0]),
     ]
@@ -679,16 +707,19 @@
     for g in range(2):
         lax.fori_loop(0, 2, functools.partial(last_stress, g), 0)
 
+    wait_all(R1R, G - 1, (rs.at[1], rr.at[1]))
+    over_x = jnp.sum(R1R[...], axis=0)
+    R2S[...] = over_x
+    R2R[gy] = over_x
+
+    def send_y(k, c):
+        sum_copy_y(k).start()
+        return c
+
+    lax.fori_loop(1, H, send_y, 0)
+
     wait_all(R2R, H - 1, (rs.at[0], rr.at[0]))
-    over_y = jnp.sum(R2R[...], axis=0)
-    R1S[...] = over_y
-    R1R[gx] = over_y
-
-    over_peers(lambda k: sum_copy_x(k).start())
-    over_peers(lambda k: out_copy(k).start(), half, G)
-
-    wait_all(R1R, G - 1, (rs.at[1], rr.at[1]))
-    res_out[...] = jnp.sum(R1R[...], axis=0)
+    res_out[...] = jnp.sum(R2R[...], axis=0)
 
     sent = F.at[:, pl.ds(24, R - 8), :]
     pltpu.make_async_copy(sent, sent, fs.at[0]).wait()
@@ -711,20 +742,25 @@
 
 
 def write_out(
-    vel_ref, stress_ref, res_ref, ocean_ref, vel_out, stress_out, res_out, ocean_out, row, sems
+    vel_ref, stress_ref, res_ref, ocean_ref, vel_out, stress_out, res_out, ocean_out,
+    row, four, sems,
 ):
+    pairs = [(res_ref, row)]
+    for src, dst in ((vel_ref, vel_out), (stress_ref, stress_out), (ocean_ref, ocean_out)):
+        pairs += [(src.at[k], dst.at[k]) for k in range(src.shape[0])]
     copies = [
-        pltpu.make_async_copy(src, dst, sems.at[k])
-        for k, (src, dst) in enumerate(
-            ((res_ref, row), (vel_ref, vel_out), (stress_ref, stress_out), (ocean_ref, ocean_out)))
+        pltpu.make_async_copy(src, dst, sems.at[k]) for k, (src, dst) in enumerate(pairs)
     ]
     for copy in copies:
         copy.start()
     copies[0].wait()
     for k in range(ITERS):
-        res_out[k] = row[0, k]
+        four[k] = row[0, k]
+    last = pltpu.make_async_copy(four, res_out, sems.at[len(copies)])
+    last.start()
     for copy in copies[1:]:
         copy.wait()
+    last.wait()
 
 
 def local(G, H, velocity, stress, ice_mass, strength, land_mask, ocean_forcing):
@@ -777,8 +813,8 @@
         out_shape=tuple(
             jax.ShapeDtypeStruct(shape, f32) for shape in (shapes[0], shapes[1], (ITERS,), shapes[3])),
         in_specs=[anywhere] * 4,
-        out_specs=(in_hbm, in_hbm, pl.BlockSpec(memory_space=pltpu.SMEM), in_hbm),
-        scratch_shapes=[pltpu.VMEM((1, 128), f32), dma((4,))],
+        out_specs=(in_hbm,) * 4,
+        scratch_shapes=[pltpu.VMEM((1, 128), f32), pltpu.SMEM((ITERS,), f32), dma((9,))],
         compiler_params=pltpu.CompilerParams(vmem_limit_bytes=1024 * 1024),
     )(*results)
 

time: 48 us -> 46.5 us (0.969)
  Pallas kernels: 47.3 us -> 45.7 us
    pallas_call x1, Pallas kernels: 45.8 us -> 44.7 us  [local(): pl.pallas_call(functools.partial(kernel, G, H), out_shape=tuple((pltpu.VM...]
where the time goes in v4:
time: 46.5 us; the launch traced here: 46.3 us
  Pallas kernels  45.7 us (98%)
  between operations  0.64 us (1%)
    pallas_call x1, Pallas kernels, local(): pl.pallas_call(functools.partial(kernel, G, H), out_shape=tuple((pltpu.VM...  44.7 us
    pallas_call x1, Pallas kernels, local(): pl.pallas_call(write_out, out_shape=tuple((jax.ShapeDtypeStruct(shape, f3...  1 us

profile of v4, /device:TPU:1, one launch (start us, length us, event | category | flops | bytes accessed | tf_op | source)
XLA Modules:
  0.0 46.3 jit_solution(13709361926116853568)
XLA Ops:
  0.6 44.7 %shard_map.93 = (f32[2,256,128]{2,1,0:T(8,128)S(1)}, f32[3,256,128]{2,1,0:T(8,128)S(1)}, f32[1,128]{1,0:T(1,128)S(1)}, f32[2,8,4096]{2,1,0:T(8,128)S(1)}) custom-call(f32[2,256,128]{2,1,0:T(8,128)} %vel_ref.1, f32[3,256,128]{2,1,0:T(8,128)} %stress_ref.1, f32[256,128]{1,0:T(8,128)} %mass_ref.1, f32[256,128]{1,0:T(8,128)} %strength_ref.1, ...), custom_call_target="tpu_custom_call" | custom-call | tf_op jit(solution)/shard_map/pallas_call | solution.py:777
  45.3 1.0 %shard_map.94 = (f32[2,256,128]{2,1,0:T(8,128)}, f32[3,256,128]{2,1,0:T(8,128)}, f32[4]{0:T(128)}, f32[2,8,4096]{2,1,0:T(8,128)}) custom-call(f32[2,256,128]{2,1,0:T(8,128)S(1)} %get-tuple-element.8.vel_ref, f32[3,256,128]{2,1,0:T(8,128)S(1)} %get-tuple-element.9.stress_ref, f32[1,128]{1,0:T(1,128)S(1)} %get-tuple-element.10.res_ref, ...), custom_call_target="tpu_custom_call" | custom-call | tf_op jit(solution)/shard_map/pallas_call | solution.py:811

commit v5 on v4

--- a/solution.py
+++ b/solution.py
@@ -109,7 +109,14 @@
         pl.semaphore_signal(bar, inc=1, device_id=(gx, peer_y(k)), device_id_type=MESH)
         return c
 
-    over_peers(greet_x)
+    greet_x(G // 2)
+
+    def greet_pair(m, c):
+        greet_x(G // 2 - m)
+        greet_x(G // 2 + m)
+        return c
+
+    lax.fori_loop(1, G // 2, greet_pair, 0)
     lax.fori_loop(1, H, greet_y, 0)
 
     @pl.when(has_south)
@@ -401,8 +408,8 @@
     def both_sums(main, strip):
         return jnp.where(main_lanes, main, 0.0) + jnp.where(strip_lanes, strip, 0.0)
 
-    main_region = (1, T + 4, 4)
-    strip_region = (strip0, S, 2)
+    main_region = (1, T + 4, 1)
+    strip_region = (strip0, S, 1)
 
     def part_row(region, c):
         first, tiles, parts = region
@@ -552,9 +559,10 @@
         own_row = 24 + part * 8 * CH
         unpack_own(8 * strip0 + 8 + part * 8 * CH, 8 * CH, own_row, own_row + R // 2)
 
-    inner = (1, 2) if NM > 2 else ()
-    for part in inner:
-        relax_part(main_region, part)
+    tiles_in = main_region[1] // main_region[2]
+    inner = [c for c in range(main_region[2]) if c * tiles_in > 2 and (c + 1) * tiles_in < T + 2]
+    if inner:
+        lax.fori_loop(inner[0], inner[-1] + 1, lambda c, _: relax_part(main_region, c), None)
 
 
     @pl.when(has_south)
@@ -571,7 +579,7 @@
     unpack_own(8 * (strip0 + S - 1), 8, 24 + R // 2, high_halo)
 
     main_sums = [main_sum]
-    for part in range(4):
+    for part in range(main_region[2]):
         if part not in inner:
             relax_part(main_region, part)
     main_sums.append(velocity_sweep(main_region, False))
@@ -647,7 +655,7 @@
 
     over_all_x(lambda p: sum_copy_x(p).start())
 
-    rows_last = 8 * CH
+    rows_last = 16 * CH
     left = lanes_between(0, 8, rows_last)
     right = lanes_between(120, 128, rows_last)
 
@@ -656,12 +664,11 @@
         x = jnp.where(left, roll(strip, -(48 * g + 8)), x)
         return jnp.where(right, roll(strip, 88 - 48 * g), x)
 
-    def last_main(g, c, carry):
-        first = pl.multiple_of(c * 8 * CH + g * R // 2, 8)
-        row = pl.multiple_of(first + 24, 8)
-        rows = pl.ds(row, rows_last)
+    def last_main(g):
+        first = g * R // 2
+        rows = pl.ds(first + 24, rows_last)
         out = pl.ds(first, rows_last)
-        strip_rows = pl.ds(pl.multiple_of((strip0 + 1) * 8 + c * 8 * CH, 8), rows_last)
+        strip_rows = pl.ds((strip0 + 1) * 8, rows_last)
         new_u = merged(X[U, rows, :], U, strip_rows, g)
         new_v = merged(X[V, rows, :], V, strip_rows, g)
         vel_out[0, out, :] = new_u
@@ -671,26 +678,24 @@
         drag = drag_of(new_u, new_v, ou, ov) * X[ICE, rows, :]
         east_stress = drag * (new_u - ou)
         north_stress = drag * (new_v - ov)
-        for t in range(CH):
-            band = c * CH + g * (T // 2) + t
+        for t in range(2 * CH):
+            band = g * (T // 2) + t
             IST[band, 0] = east_stress[8 * t:8 * t + 8]
             IST[band, 1] = north_stress[8 * t:8 * t + 8]
-        return carry
-
-    def last_stress(g, c, carry):
-        first = pl.multiple_of(c * 8 * CH + g * R // 2, 8)
-        rows = pl.ds(pl.multiple_of(first + 24, 8), rows_last)
+
+    def last_stress(g):
+        first = g * R // 2
+        rows = pl.ds(first + 24, rows_last)
         out = pl.ds(first, rows_last)
-        strip_rows = pl.ds(pl.multiple_of((strip0 + 1) * 8 + c * 8 * CH, 8), rows_last)
+        strip_rows = pl.ds((strip0 + 1) * 8, rows_last)
         a = merged(X[A, rows, :], A, strip_rows, g)
         b = merged(X[B, rows, :], B, strip_rows, g)
         stress_out[0, out, :] = 2.0 * (a + b)
         stress_out[1, out, :] = 2.0 * (a - b)
         stress_out[2, out, :] = 2.0 * merged(X[C, rows, :], C, strip_rows, g)
-        return carry
 
     for g in range(2):
-        lax.fori_loop(0, 2, functools.partial(last_main, g), 0)
+        last_main(g)
 
     def out_copy(p):
         return pltpu.make_async_remote_copy(
@@ -705,7 +710,7 @@
         store.start()
 
     for g in range(2):
-        lax.fori_loop(0, 2, functools.partial(last_stress, g), 0)
+        last_stress(g)
 
     wait_all(R1R, G - 1, (rs.at[1], rr.at[1]))
     over_x = jnp.sum(R1R[...], axis=0)

time: 46.5 us -> 45.1 us (0.970)
  Pallas kernels: 45.7 us -> 44.3 us
    pallas_call x1, Pallas kernels: 44.7 us -> 43.3 us  [local(): pl.pallas_call(functools.partial(kernel, G, H), out_shape=tuple((pltpu.VM...]
where the time goes in v5:
time: 45.1 us; the launch traced here: 44.9 us
  Pallas kernels  44.3 us (98%)
  between operations  0.64 us (1%)
    pallas_call x1, Pallas kernels, local(): pl.pallas_call(functools.partial(kernel, G, H), out_shape=tuple((pltpu.VM...  43.3 us
    pallas_call x1, Pallas kernels, local(): pl.pallas_call(write_out, out_shape=tuple((jax.ShapeDtypeStruct(shape, f3...  1 us

profile of v5, /device:TPU:1, one launch (start us, length us, event | category | flops | bytes accessed | tf_op | source)
XLA Modules:
  0.0 44.9 jit_solution(12216577597385671204)
XLA Ops:
  0.6 43.3 %shard_map.93 = (f32[2,256,128]{2,1,0:T(8,128)S(1)}, f32[3,256,128]{2,1,0:T(8,128)S(1)}, f32[1,128]{1,0:T(1,128)S(1)}, f32[2,8,4096]{2,1,0:T(8,128)S(1)}) custom-call(f32[2,256,128]{2,1,0:T(8,128)} %vel_ref.1, f32[3,256,128]{2,1,0:T(8,128)} %stress_ref.1, f32[256,128]{1,0:T(8,128)} %mass_ref.1, f32[256,128]{1,0:T(8,128)} %strength_ref.1, ...), custom_call_target="tpu_custom_call" | custom-call | tf_op jit(solution)/shard_map/pallas_call | solution.py:782
  43.9 1.0 %shard_map.94 = (f32[2,256,128]{2,1,0:T(8,128)}, f32[3,256,128]{2,1,0:T(8,128)}, f32[4]{0:T(128)}, f32[2,8,4096]{2,1,0:T(8,128)}) custom-call(f32[2,256,128]{2,1,0:T(8,128)S(1)} %get-tuple-element.8.vel_ref, f32[3,256,128]{2,1,0:T(8,128)S(1)} %get-tuple-element.9.stress_ref, f32[1,128]{1,0:T(1,128)S(1)} %get-tuple-element.10.res_ref, ...), custom_call_target="tpu_custom_call" | custom-call | tf_op jit(solution)/shard_map/pallas_call | solution.py:816

commit v6 on v5

--- a/solution.py
+++ b/solution.py
@@ -254,7 +254,14 @@
         forcing_copy(G // 2 + m).start()
         return c
 
-    lax.fori_loop(1, G // 2, send_pair, 0)
+    near = max(G // 2 - 4, 1)
+    held = gy - gy // 2 * 2 == 1
+    lax.fori_loop(1, near, send_pair, 0)
+
+    @pl.when(jnp.logical_not(held))
+    def _():
+        lax.fori_loop(near, G // 2, send_pair, 0)
+
 
     @pl.when(has_south)
     def _():
@@ -455,6 +462,10 @@
     stress_sweep(main_region)
     stress_sweep(strip_region)
 
+    @pl.when(held)
+    def _():
+        lax.fori_loop(near, G // 2, send_pair, 0)
+
     def wait_bands(sem, row, count):
         where = F.at[:, pl.ds(row, 8 * count), :]
         pltpu.make_async_copy(where, where, fr.at[sem]).wait()
@@ -512,16 +523,18 @@
     at_home = jnp.where((gx == 0) | (gx == G - 1), 0, 1)
 
     def receive(step, acc):
-        @pl.when(step == jnp.maximum(home - 1, 0))
+        beside = jnp.where(home == 3, 3 - 2 * (step - 1), 1 + 2 * (step - 1))
+        chunk = home + jnp.where(step == 0, 2, jnp.where(step == 3, 0, beside))
+        chunk = jnp.where(chunk >= 4, chunk - 4, chunk)
+
+        @pl.when(chunk == 0)
         def _():
             pass_on(True)
 
-        @pl.when(step == home)
+        @pl.when(chunk == 3)
         def _():
             pass_on(False)
 
-        chunk = home + 3 - step
-        chunk = jnp.where(chunk >= 4, chunk - 4, chunk)
         row = pl.multiple_of(chunk * 8 * CH + 24, 8)
         missing = (
             jnp.where(chunk == 0, 1, 0) + jnp.where(chunk == 3, 1, 0)

time: 45.1 us -> 44.6 us (0.989)
  Pallas kernels: 44.3 us -> 43.8 us
    pallas_call x1, Pallas kernels: 43.3 us -> 42.8 us  [local(): pl.pallas_call(functools.partial(kernel, G, H), out_shape=tuple((pltpu.VM...]
where the time goes in v6:
time: 44.6 us; the launch traced here: 44.5 us
  Pallas kernels  43.8 us (98%)
  between operations  0.64 us (1%)
    pallas_call x1, Pallas kernels, local(): pl.pallas_call(functools.partial(kernel, G, H), out_shape=tuple((pltpu.VM...  42.8 us
    pallas_call x1, Pallas kernels, local(): pl.pallas_call(write_out, out_shape=tuple((jax.ShapeDtypeStruct(shape, f3...  1 us

profile of v6, /device:TPU:1, one launch (start us, length us, event | category | flops | bytes accessed | tf_op | source)
XLA Modules:
  0.0 44.5 jit_solution(17615743191838560259)
XLA Ops:
  0.6 42.8 %shard_map.93 = (f32[2,256,128]{2,1,0:T(8,128)S(1)}, f32[3,256,128]{2,1,0:T(8,128)S(1)}, f32[1,128]{1,0:T(1,128)S(1)}, f32[2,8,4096]{2,1,0:T(8,128)S(1)}) custom-call(f32[2,256,128]{2,1,0:T(8,128)} %vel_ref.1, f32[3,256,128]{2,1,0:T(8,128)} %stress_ref.1, f32[256,128]{1,0:T(8,128)} %mass_ref.1, f32[256,128]{1,0:T(8,128)} %strength_ref.1, ...), custom_call_target="tpu_custom_call" | custom-call | tf_op jit(solution)/shard_map/pallas_call | solution.py:795
  43.5 1.0 %shard_map.94 = (f32[2,256,128]{2,1,0:T(8,128)}, f32[3,256,128]{2,1,0:T(8,128)}, f32[4]{0:T(128)}, f32[2,8,4096]{2,1,0:T(8,128)}) custom-call(f32[2,256,128]{2,1,0:T(8,128)S(1)} %get-tuple-element.8.vel_ref, f32[3,256,128]{2,1,0:T(8,128)S(1)} %get-tuple-element.9.stress_ref, f32[1,128]{1,0:T(1,128)S(1)} %get-tuple-element.10.res_ref, ...), custom_call_target="tpu_custom_call" | custom-call | tf_op jit(solution)/shard_map/pallas_call | solution.py:829
